TPU v7x, 32 devices: a whole 2x2x4 slice. The times are simulated.
32 devices in a mesh: seq: 8 (over z, core), tp: 2 (over y), dp: 2 (over x).
Axes of the slice: x: 2, y: 2, z: 4, core: 2. Of those that a mesh axis runs over, the one named last changes fastest.
Arguments:
- query_latent: bfloat16 [2, 2048, 1536], P('dp', 'seq', 'tp'), may hold values from -6 to 6
- key_latent: bfloat16 [2, 2048, 512], P('dp', 'seq', 'tp'), may hold values from -6 to 6
- rope_key: bfloat16 [2, 2048, 64], P('dp', 'seq'), may hold values from -6 to 6
- w_uq: bfloat16 [1536, 12288], P('seq', 'tp')
- w_uk: bfloat16 [512, 8192], P('seq', 'tp'), may hold values from -0.25 to 0.25
- w_uv: bfloat16 [512, 8192], P('seq', 'tp'), may hold values from -0.25 to 0.25
- block_order: int32 [2, 16], P('dp'), may hold values from 0 to 15, each once within a row
- segment_ids: int32 [2, 2048], P('dp'), may hold values from 0 to 3, never falling along the last dimension, each value on 1 to 1024 neighbouring positions
Outputs:
- context: bfloat16 [2, 2048, 8192], P('dp', 'seq', 'tp')
- clipped_uq: bfloat16 [1536, 12288], P('seq', 'tp')
- clipped_uk: bfloat16 [512, 8192], P('seq', 'tp')
Inputs may be any that keep to these rules, and one draw needn't show every extreme that they name: `block_order`: each row is a permutation of the 16 position blocks. `segment_ids`: never falling along positions; each document has at most 1024 positions.
All inputs are finite; a program needn't handle non-finite values.
Results may differ from a plain program's by a relative error of at most 0.012.
The roundings to bfloat16 on the way count: a program that leaves them out, or rounds other values in their place, can miss the bound.
Values may be sent and summed in bfloat16 or wider, within the bound.
A program may use at most 128 MiB of HBM per device.

v0:
```python
import functools
import math

import jax
import jax.numpy as jnp
import numpy as np
from jax import lax
from jax.experimental import pallas as pl
from jax.experimental.pallas import tpu as pltpu
from jax.sharding import PartitionSpec as P

NOPE = 128
ROPE = 64
VD = 128
CLIP = 8


rope_base = 50000.0
masked_value = -1e30


def turning(positions, width):
    steps = jnp.arange(width // 2, dtype=jnp.float32) * (2.0 / width)
    freqs = jnp.exp(-math.log(rope_base) * steps)
    angle = positions.astype(jnp.float32)[:, None] * freqs[None, :]
    return (jnp.cos(angle), jnp.sin(angle))


def rotate(values, cosine, sine):
    half = values.shape[-1] // 2
    first = values[..., :half]
    second = values[..., half:]
    return jnp.concatenate(
        [first * cosine - second * sine, second * cosine + first * sine], axis=-1
    )


def positions_of(index, order, half_block):
    which = index // half_block
    onehot = which[:, None] == jnp.arange(order.shape[0], dtype=jnp.int32)[None, :]
    base = jnp.sum(jnp.where(onehot, order[None, :], 0), axis=1)
    return base * half_block + index % half_block


def by_tokens(query_latent, key_latent, rope_key, w_uq, w_uk, w_uv, block_order, segment_ids):
    query_local, key_local = (
        lax.all_gather(query_latent[0], "tp", axis=1, tiled=True),
        lax.all_gather(key_latent[0], "tp", axis=1, tiled=True),
    )
    rows_uq, rows_uk, rows_uv = (
        lax.all_gather(w_uq, "seq", axis=0, tiled=True),
        lax.all_gather(w_uk, "seq", axis=0, tiled=True),
        lax.all_gather(w_uv, "seq", axis=0, tiled=True),
    )
    tok_rows = query_local.shape[0]
    half_block = tok_rows // 2
    order = block_order[0]
    labels_all = segment_ids[0]
    heads = w_uq.shape[1] // (NOPE + ROPE)
    scale = 1.0 / math.sqrt(NOPE + ROPE)
    own_index = lax.axis_index("seq") * tok_rows + jnp.arange(tok_rows, dtype=jnp.int32)
    query_pos = positions_of(own_index, order, half_block)
    query_labels = jnp.take(labels_all, query_pos)
    cosine, sine = turning(query_pos, ROPE)
    query_full = jnp.dot(query_local, rows_uq, preferred_element_type=jnp.float32).reshape(
        tok_rows, heads, NOPE + ROPE
    )
    query_nope = jnp.transpose(query_full[:, :, :NOPE].astype(jnp.bfloat16), (1, 0, 2))
    query_rope = jnp.transpose(
        rotate(query_full[:, :, NOPE:], cosine[:, None, :], sine[:, None, :]).astype(jnp.bfloat16),
        (1, 0, 2),
    )
    key_rope = rotate(rope_key[0].astype(jnp.float32), cosine, sine).astype(jnp.bfloat16)

    def slice_latent(pieces, first, width):
        latent_block = lax.dynamic_slice_in_dim(pieces[0], first, width, 0)
        rope_block = lax.dynamic_slice_in_dim(pieces[1], first, width, 0)
        nope_block = jnp.dot(latent_block, rows_uk, preferred_element_type=jnp.float32).astype(
            jnp.bfloat16
        )
        value_block = jnp.dot(latent_block, rows_uv, preferred_element_type=jnp.float32).astype(
            jnp.bfloat16
        )
        return (nope_block, value_block, rope_block)

    initial = (
        jnp.full((heads, tok_rows), masked_value, jnp.float32),
        jnp.zeros((heads, tok_rows), jnp.float32),
        jnp.zeros((heads, tok_rows, VD), jnp.float32),
    )
    pieces = (
        lax.all_gather(key_local, "seq", axis=0, tiled=True),
        lax.all_gather(key_rope, "seq", axis=0, tiled=True),
    )
    count = pieces[-1].shape[0]
    width = math.gcd(count, 512)

    def block_step(state, number):
        first = number * width
        nope_block, value_block, rope_block = slice_latent(pieces, first, width)
        nope_block = nope_block.reshape(width, heads, NOPE)
        value_block = value_block.reshape(width, heads, VD)
        key_index = first + jnp.arange(width, dtype=jnp.int32)
        key_pos = positions_of(key_index, order, half_block)
        key_labels = jnp.take(labels_all, key_pos)
        allowed = (key_pos[None, :] <= query_pos[:, None]) & (
            key_labels[None, :] == query_labels[:, None]
        )
        scores = jnp.einsum(
            "hqd,khd->hqk", query_nope, nope_block, preferred_element_type=jnp.float32
        )
        scores = (
            scores
            + jnp.einsum("hqr,kr->hqk", query_rope, rope_block, preferred_element_type=jnp.float32)
        ) * scale
        masked = jnp.where(allowed[None], scores, masked_value)
        run_max, run_total, run_sum = state
        new_max = jnp.maximum(run_max, jnp.max(masked, axis=2))
        weights = jnp.where(allowed[None], jnp.exp(masked - new_max[:, :, None]), 0.0)
        shrink = jnp.exp(run_max - new_max)
        new_total = run_total * shrink + jnp.sum(weights, axis=2)
        mixed = jnp.einsum(
            "hqk,khv->hqv",
            weights.astype(jnp.bfloat16),
            value_block,
            preferred_element_type=jnp.float32,
        )
        new_sum = run_sum * shrink[:, :, None] + mixed
        return ((new_max, new_total, new_sum), None)

    result, unused = lax.scan(block_step, initial, jnp.arange(count // width, dtype=jnp.int32))
    run_max, run_total, run_sum = result
    context = (run_sum / run_total[:, :, None]).astype(jnp.bfloat16)
    context = jnp.transpose(context, (1, 0, 2)).reshape(1, tok_rows, heads * VD)
    head_max = lax.pmax(jnp.max(run_max, axis=1), ("seq", "dp"))
    ratio = CLIP / jnp.maximum(head_max, CLIP)
    root = jnp.sqrt(ratio)
    factors = jnp.concatenate(
        [
            jnp.broadcast_to(root[:, None], (heads, NOPE)),
            jnp.broadcast_to(ratio[:, None], (heads, ROPE)),
        ],
        axis=1,
    ).reshape(heads * (NOPE + ROPE))
    clipped_uq = (w_uq.astype(jnp.float32) * factors[None, :]).astype(jnp.bfloat16)
    clipped_uk = (w_uk.astype(jnp.float32) * jnp.repeat(root, NOPE)[None, :]).astype(jnp.bfloat16)
    return (context, clipped_uq, clipped_uk)


def turned(values, cosine, sine):
    half = values.shape[-1] // 2
    swapped = jnp.concatenate([values[:, half:], values[:, :half]], axis=1)
    return values * cosine + swapped * sine


def attend(
    block, tile, own, order, labels,
    query_ref, key_ref, rope_ref, wq_ref, wk_ref, wv_ref, turn_ref, row_ref,
    context_ref, peak_ref,
    q_s, k_s, v_s, s_s, m_s, stored_at,
):
    count = query_ref.shape[0]
    scale = 1.0 / math.sqrt(NOPE + ROPE)
    width = NOPE + ROPE
    rows = min(count, 4 * block)
    for stored in range(count // block):
        stored_at[order[stored]] = stored

    def project(step, unused):
        at = pl.multiple_of(step * rows, rows)
        latent = key_ref[pl.ds(at, rows), :]
        nope = jnp.dot(latent, wk_ref[...], preferred_element_type=jnp.float32).astype(jnp.bfloat16)
        value = jnp.dot(latent, wv_ref[...], preferred_element_type=jnp.float32).astype(jnp.bfloat16)
        full = jnp.dot(
            query_ref[pl.ds(at, rows), :], wq_ref[...], preferred_element_type=jnp.float32
        )
        for part in range(rows // block):
            lo, hi = part * block, (part + 1) * block
            to = pl.multiple_of(order[step * (rows // block) + part] * block, block)
            there = pl.ds(to, block)
            cosine, sine = turn_ref[there, :ROPE], turn_ref[there, ROPE:]
            raw = rope_ref[pl.ds(pl.multiple_of(at + lo, block), block), :].astype(jnp.float32)
            key_rope = turned(raw, cosine, sine).astype(jnp.bfloat16)
            v_s[there, :] = value[lo:hi, :]
            for head in range(own):
                base = head * width
                k_s[head, there, :NOPE] = nope[lo:hi, head * NOPE : (head + 1) * NOPE]
                k_s[head, there, NOPE:] = key_rope
                q_s[head, there, :NOPE] = full[lo:hi, base : base + NOPE].astype(jnp.bfloat16)
                q_s[head, there, NOPE:] = turned(
                    full[lo:hi, base + NOPE : base + width], cosine, sine
                ).astype(jnp.bfloat16)
        return unused

    lax.fori_loop(0, count // rows, project, 0)

    def per_tile(number, best):
        opening = labels[number * tile]
        first = sum(
            (labels[(chunk + 1) * tile - 1] < opening).astype(jnp.int32)
            for chunk in range(count // tile)
        )
        own_labels = jnp.transpose(jnp.broadcast_to(row_ref[number], (tile, tile)))
        here = pl.ds(pl.multiple_of(number * tile, tile), tile)
        for head in range(own):
            m_s[head] = jnp.full((tile, 128), masked_value, jnp.float32)

        def score(chunk, unused):
            there = pl.ds(pl.multiple_of(chunk * tile, tile), tile)
            gap = (chunk - number) * tile
            later = lax.broadcasted_iota(jnp.int32, (tile, tile), 1) + gap
            now = lax.broadcasted_iota(jnp.int32, (tile, tile), 0)
            allowed = (later <= now) & (own_labels == row_ref[chunk])
            for head in range(own):
                raw = lax.dot_general(
                    q_s[head, here, :], k_s[head, there, :], (((1,), (1,)), ((), ())),
                    preferred_element_type=jnp.float32,
                )
                raw = jnp.where(allowed, raw, masked_value)
                s_s[chunk - first, head] = raw
                best_here = m_s[head]
                for lane in range(tile // 128):
                    best_here = jnp.maximum(best_here, raw[:, lane * 128 : (lane + 1) * 128])
                m_s[head] = best_here
            return unused

        lax.fori_loop(first, number + 1, score, 0)
        tops = []
        for head in range(own):
            top = jnp.max(m_s[head], axis=1, keepdims=True)
            m_s[head] = jnp.broadcast_to(top, (tile, 128))
            tops.append(jnp.broadcast_to(jnp.max(top, axis=0, keepdims=True), (1, 128)))

        factor = scale * math.log2(math.e)

        def mix(chunk, state):
            there = pl.ds(pl.multiple_of(chunk * tile, tile), tile)
            out = []
            for head in range(own):
                total, mixed = state[head]
                top = m_s[head]
                raw = s_s[chunk - first, head]
                pieces = [
                    jnp.exp2((raw[:, lane * 128 : (lane + 1) * 128] - top) * factor)
                    for lane in range(tile // 128)
                ]
                for piece in pieces:
                    total = total + piece
                weights = jnp.concatenate([piece.astype(jnp.bfloat16) for piece in pieces], axis=1)
                mixed = mixed + jnp.dot(
                    weights, v_s[there, head * VD : (head + 1) * VD],
                    preferred_element_type=jnp.float32,
                )
                out.append((total, mixed))
            return tuple(out)

        zero = tuple(
            (jnp.zeros((tile, 128), jnp.float32), jnp.zeros((tile, VD), jnp.float32))
            for head in range(own)
        )
        state = lax.fori_loop(first, number + 1, mix, zero)
        for head in range(own):
            total, mixed = state[head]
            done = (mixed / jnp.sum(total, axis=1, keepdims=True)).astype(jnp.bfloat16)
            for part in range(tile // block):
                to = pl.multiple_of(stored_at[number * (tile // block) + part] * block, block)
                context_ref[pl.ds(to, block), head * VD : (head + 1) * VD] = done[
                    part * block : (part + 1) * block, :
                ]
        return jnp.maximum(best, jnp.concatenate(tops, axis=0))

    best = lax.fori_loop(
        0, count // tile, per_tile, jnp.full((own, 128), masked_value, jnp.float32)
    )
    peak_ref[...] = best * scale


MESH = pl.DeviceIdType.MESH


def window(start, size):
    return pl.ds(pl.multiple_of(start * size, size), size)


def greet(wheres):
    barrier = pltpu.get_barrier_semaphore()
    for where in wheres:
        pl.semaphore_signal(barrier, inc=1, device_id=where, device_id_type=MESH)
    pl.semaphore_wait(barrier, len(wheres))


def spread(
    n, query_ref, key_ref, rope_ref, uq_ref, uk_ref, uv_ref,
    query_out, key_out, rope_out, wq_out, wk_out, wv_out,
    sends, got_query, got_key, got_rope, got_weight, local,
):
    s, t, d = lax.axis_index("seq"), lax.axis_index("tp"), lax.axis_index("dp")
    partner = s + 1 - 2 * lax.rem(s, 2)
    parity, level, levels = lax.rem(s, 2), s // 2, n // 2
    same = lambda z: 2 * z + parity
    cross = lambda z: 2 * z + 1 - parity
    turn = lambda k: lax.rem(level + k, levels)
    within = lambda z: (z >= 0) & (z < levels)
    beside, across, mate = {"tp": 1 - t}, {"dp": 1 - d}, {"seq": partner}
    greet(
        [mate, beside, across]
        + [{"seq": same(turn(k))} for k in range(1, levels)]
        + [{"seq": cross(turn(k))} for k in range(1, levels)]
    )
    rows, wide = query_ref.shape
    thin = key_ref.shape[1]
    weights = ((uq_ref, wq_out), (uk_ref, wk_out), (uv_ref, wv_out))
    state = {"when": None}
    started = []

    def link(source, target, arrived, where, sender):
        return pltpu.make_async_remote_copy(
            src_ref=source, dst_ref=target, send_sem=sends.at[sender], recv_sem=arrived,
            device_id=where, device_id_type=MESH,
        )

    def send(source, target, arrived, where):
        link(source, target, arrived, where, len(started)).start()
        started.append((tuple(source.shape), state["when"]))

    def under(condition, action):
        state["when"] = condition
        pl.when(condition)(action)
        state["when"] = None

    def arrive(target, arrived):
        link(target, target, arrived, mate, 0).wait_recv()

    def spots(src, tp):
        return (
            (query_out.at[window(src, rows), window(tp, wide)], got_query.at[src, tp]),
            (key_out.at[window(src, rows), window(tp, thin)], got_key.at[src, tp]),
        )

    def rope_spot(src):
        return (rope_out.at[window(src, rows), :], got_rope.at[src])

    def own_latents(where, rope):
        for source, (target, arrived) in zip((query_ref, key_ref), spots(s, t)):
            send(source, target, arrived, where)
        if rope:
            send(rope_ref, *rope_spot(s), where)

    def await_latents(src, tp, rope):
        for target, arrived in spots(src, tp):
            arrive(target, arrived)
        if rope:
            arrive(*rope_spot(src))

    def pass_latents(src, tp, where, rope):
        for target, arrived in spots(src, tp):
            send(target, target, arrived, where)
        if rope:
            target, arrived = rope_spot(src)
            send(target, target, arrived, where)

    def weight_spot(index, src, half):
        out = weights[index][1]
        depth = weights[index][0].shape[0] // 2
        return (out.at[window(src * 2 + half, depth), :], got_weight.at[index, src, half])

    def own_weights(to):
        for index, (ref, out) in enumerate(weights):
            piece = ref.at[window(d, ref.shape[0] // 2), window(to, out.shape[1])]
            send(piece, *weight_spot(index, s, d), {"seq": to})

    def pass_weights(src):
        for index in range(len(weights)):
            target, arrived = weight_spot(index, src, d)
            arrive(target, arrived)
            send(target, target, arrived, across)

    own_latents(beside, False)
    for sign in (1, -1):
        to = level + sign
        under(within(to), lambda: own_latents({"seq": same(to)}, True))
    own_latents(mate, True)
    own_weights(partner)
    kept = [
        pltpu.make_async_copy(source, target, local.at[place])
        for place, (source, target) in enumerate(
            [(query_ref, spots(s, t)[0][0]), (key_ref, spots(s, t)[1][0]), (rope_ref, rope_spot(s)[0])]
            + [
                (ref.at[:, window(s, out.shape[1])], out.at[window(s, ref.shape[0]), :])
                for ref, out in weights
            ]
        )
    ]
    for copy in kept:
        copy.start()

    def from_beside(k):
        for sign in (1, -1) if k else (1,):
            source = level - sign * k

            def hand():
                await_latents(same(source), 1 - t, False)
                pass_latents(same(source), 1 - t, mate, False)

            under(within(source), hand)

    for k in range(1, levels):
        for sign in (1, -1):
            to = level + sign * k

            def far():
                own_weights(same(to))
                own_weights(cross(to))

            under(within(to), far)
        for sign in (1, -1):
            source, onward = level - sign * k, level + sign

            def take():
                await_latents(same(source), t, True)
                pass_latents(same(source), t, beside, False)
                pass_latents(same(source), t, mate, True)

            under(within(source), take)
            under(
                within(source) & within(onward),
                lambda: pass_latents(same(source), t, {"seq": same(onward)}, True),
            )
        if k == 1:
            pass_weights(partner)
        for sign in (1, -1):
            source = level - sign * k

            def relay():
                pass_weights(same(source))
                pass_weights(cross(source))

            under(within(source), relay)
        from_beside(k - 1)
    from_beside(levels - 1)
    for k in range(levels):
        await_latents(cross(turn(k)), t, True)
        await_latents(cross(turn(k)), 1 - t, False)
    for k in range(levels):
        for src in [cross(turn(k))] + ([same(turn(k))] if k else []):
            for index in range(len(weights)):
                arrive(*weight_spot(index, src, 1 - d))
    alike = [target for target, _ in spots(s, t)] + [rope_spot(s)[0]]
    alike += [weight_spot(index, s, d)[0] for index in range(len(weights))]
    alike = {tuple(ref.shape): ref for ref in alike}
    for sender, (shape, condition) in enumerate(started):
        sent = link(alike[shape], alike[shape], got_rope.at[s], mate, sender)
        if condition is None:
            sent.wait_send()
        else:
            pl.when(condition)(sent.wait_send)
    for copy in kept:
        copy.wait()


def give_back(n, context_ref, peak_ref, out_ref, peaks_ref, sends, got_context, got_peak, local):
    s, d = lax.axis_index("seq"), lax.axis_index("dp")
    rows, wide = out_ref.shape[0], context_ref.shape[1]
    steps = [k for k in range(1, n)]
    peers = [lax.rem(s + k, n) for k in steps]
    wheres = [{"seq": to} for to in peers]
    others = [{"dp": 1 - d}] + [{"seq": to, "dp": 1 - d} for to in peers]
    greet(wheres + others)
    started = []

    def link(source, target, arrived, where, sender):
        return pltpu.make_async_remote_copy(
            src_ref=source, dst_ref=target, send_sem=sends.at[sender], recv_sem=arrived,
            device_id=where, device_id_type=MESH,
        )

    def send(source, target, arrived, where):
        copy = link(source, target, arrived, where, len(started))
        copy.start()
        started.append(copy)

    me = d * n + s
    for where in wheres + others:
        send(peak_ref, peaks_ref.at[me], got_peak.at[me], where)
    for to, where in zip(peers, wheres):
        send(context_ref.at[window(to, rows), :], out_ref.at[:, window(s, wide)], got_context.at[s], where)
    kept = [
        pltpu.make_async_copy(peak_ref, peaks_ref.at[me], local.at[0]),
        pltpu.make_async_copy(context_ref.at[window(s, rows), :], out_ref.at[:, window(s, wide)], local.at[1]),
    ]
    for copy in kept:
        copy.start()
    for src in peers:
        target = out_ref.at[:, window(src, wide)]
        link(target, target, got_context.at[src], wheres[0], 0).wait_recv()
    for src in [d * n + p for p in peers] + [(1 - d) * n + p for p in peers] + [(1 - d) * n + s]:
        link(peaks_ref.at[src], peaks_ref.at[src], got_peak.at[src], wheres[0], 0).wait_recv()
    for copy in started:
        copy.wait_send()
    for copy in kept:
        copy.wait()


def by_heads(query_latent, key_latent, rope_key, w_uq, w_uk, w_uv, block_order, segment_ids):
    devices = lax.axis_size("seq")
    heads = w_uq.shape[1] // (NOPE + ROPE)
    own = heads // devices
    anyplace = pl.BlockSpec(memory_space=pl.ANY)
    vmem = pl.BlockSpec(memory_space=pltpu.VMEM)
    smem = pl.BlockSpec(memory_space=pltpu.SMEM)
    sides = lax.axis_size("tp")
    rows = query_latent.shape[1]
    shapes = (
        (devices * rows, sides * query_latent.shape[2]),
        (devices * rows, sides * key_latent.shape[2]),
        (devices * rows, ROPE),
        (devices * w_uq.shape[0], w_uq.shape[1] // devices),
        (devices * w_uk.shape[0], w_uk.shape[1] // devices),
        (devices * w_uv.shape[0], w_uv.shape[1] // devices),
    )
    half = devices // 2
    copies = 44 * half
    query, key, rope, wq, wk, wv = pl.pallas_call(
        functools.partial(spread, devices),
        out_shape=[jax.ShapeDtypeStruct(shape, jnp.bfloat16) for shape in shapes],
        in_specs=[anyplace] * 6,
        out_specs=[anyplace] * 6,
        scratch_shapes=[
            pltpu.SemaphoreType.DMA((copies,)),
            pltpu.SemaphoreType.DMA((devices, sides)),
            pltpu.SemaphoreType.DMA((devices, sides)),
            pltpu.SemaphoreType.DMA((devices,)),
            pltpu.SemaphoreType.DMA((3, devices, 2)),
            pltpu.SemaphoreType.DMA((6,)),
        ],
        compiler_params=pltpu.CompilerParams(collective_id=0, has_side_effects=True),
        cost_estimate=pl.CostEstimate(
            flops=30_000_000_000, bytes_accessed=16_000_000, transcendentals=0
        ),
        name="spread",
    )(query_latent[0], key_latent[0], rope_key[0], w_uq, w_uk, w_uv)
    order, labels = block_order[0], segment_ids[0]
    count, blocks = labels.shape[0], order.shape[0]
    block = count // blocks
    tile = 2 * block
    chunks = count // tile
    steps = np.arange(ROPE // 2, dtype=np.float32) * np.float32(2.0 / ROPE)
    freqs = np.exp(np.float32(-math.log(rope_base)) * steps).astype(np.float32)
    angle = np.arange(count, dtype=np.float32)[:, None] * freqs[None, :]
    cosine, sine = np.cos(angle), np.sin(angle)
    turns = jnp.asarray(np.concatenate([cosine, cosine, -sine, sine], axis=1), jnp.float32)
    context, peak = pl.pallas_call(
        functools.partial(attend, block, tile, own),
        out_shape=(
            jax.ShapeDtypeStruct((count, own * VD), jnp.bfloat16),
            jax.ShapeDtypeStruct((own, 128), jnp.float32),
        ),
        in_specs=[smem] * 2 + [vmem] * 8,
        out_specs=(vmem, vmem),
        scratch_shapes=[
            pltpu.VMEM((own, count, NOPE + ROPE), jnp.bfloat16),
            pltpu.VMEM((own, count, NOPE + ROPE), jnp.bfloat16),
            pltpu.VMEM((count, own * VD), jnp.bfloat16),
            pltpu.VMEM((chunks, own, tile, tile), jnp.float32),
            pltpu.VMEM((own, tile, 128), jnp.float32),
            pltpu.SMEM((blocks,), jnp.int32),
        ],
        compiler_params=pltpu.CompilerParams(vmem_limit_bytes=60 * 1024 * 1024),
        cost_estimate=pl.CostEstimate(
            flops=12_000_000_000, bytes_accessed=16_000_000, transcendentals=4_000_000
        ),
        name="attend",
    )(
        order, labels, query, key, rope, wq, wk, wv, turns, labels.reshape(chunks, 1, tile),
    )
    context, peaks = pl.pallas_call(
        functools.partial(give_back, devices),
        out_shape=[
            jax.ShapeDtypeStruct((rows, heads * VD), jnp.bfloat16),
            jax.ShapeDtypeStruct((2 * devices, own, 128), jnp.float32),
        ],
        in_specs=[anyplace, vmem],
        out_specs=[anyplace, vmem],
        scratch_shapes=[
            pltpu.SemaphoreType.DMA((3 * devices,)),
            pltpu.SemaphoreType.DMA((devices,)),
            pltpu.SemaphoreType.DMA((2 * devices,)),
            pltpu.SemaphoreType.DMA((2,)),
        ],
        compiler_params=pltpu.CompilerParams(collective_id=1, has_side_effects=True),
        name="give_back",
    )(context, peak)
    head_max = jnp.max(peaks[:, :, 0].reshape(2, heads), axis=0)
    return (context[None],) + clipped(w_uq, w_uk, head_max, heads)


def clipped(w_uq, w_uk, head_max, heads):
    ratio = CLIP / jnp.maximum(head_max, CLIP)
    root = jnp.sqrt(ratio)
    factors = jnp.concatenate(
        [
            jnp.broadcast_to(root[:, None], (heads, NOPE)),
            jnp.broadcast_to(ratio[:, None], (heads, ROPE)),
        ],
        axis=1,
    ).reshape(heads * (NOPE + ROPE))
    clipped_uq = (w_uq.astype(jnp.float32) * factors[None, :]).astype(jnp.bfloat16)
    clipped_uk = (w_uk.astype(jnp.float32) * jnp.repeat(root, NOPE)[None, :]).astype(jnp.bfloat16)
    return (clipped_uq, clipped_uk)


def on_device(*arrays):
    heads = arrays[3].shape[1] // (NOPE + ROPE)
    pairs = lax.axis_size("tp") == 2 and lax.axis_size("dp") == 2
    if pairs and heads % (2 * lax.axis_size("seq")) == 0:
        return by_heads(*arrays)
    return by_tokens(*arrays)


def solution(mesh):
    placed = (
        P("dp", "seq", "tp"),
        P("dp", "seq", "tp"),
        P("dp", "seq", None),
        P("seq", "tp"),
        P("seq", "tp"),
        P("seq", "tp"),
        P("dp", None),
        P("dp", None),
    )
    return jax.shard_map(
        on_device,
        mesh=mesh,
        in_specs=placed,
        out_specs=(P("dp", "seq", "tp"), P("seq", "tp"), P("seq", "tp")),
        check_vma=False,
    )
```

profile of v0, /device:TPU:13, one launch (start us, length us, event | category | flops | bytes accessed | tf_op | source)
XLA Modules:
  0.0 197.2 jit_solution(7506039145441174907)
XLA Ops:
  0.6 1.5 copy.13
  2.1 80.6 %spread.1 = (bf16[2048,1536]{1,0:T(8,128)(2,1)}, bf16[2048,512]{1,0:T(8,128)(2,1)}, bf16[2048,64]{1,0:T(8,128)(2,1)}, bf16[1536,768]{1,0:T(8,128)(2,1)}, bf16[51...) custom-call(bf16[256,768]{1,0:T(8,128)(2,1)} %bitcast.11, bf16[256,256]{1,0:T(8,128)(2,1)} %bitcast.12, ...), custom_call_target="tpu_custom_call" | custom-call | flops 30000001024 | bytes 16000000 | tf_op jit(solution)/shard_map/spread/pallas_call | solution.py:523
  82.7 0.0 copy-start.2
  82.7 36.8 %attend.1 = (bf16[2048,512]{1,0:T(8,128)(2,1)}, f32[4,128]{1,0:T(4,128)}) custom-call(s32[16]{0:T(128)} %bitcast.15, s32[2048]{0:T(1024)} %bitcast.13, bf16[2048,1536]{1,0:T(8,128)(2,1)} %get-tuple-element.13.query_ref, bf16[2048,512]{1,0:T(8,128)(2,1)} %get-tuple-element.14.key_ref, bf16[2048,64]{1,0:T(8,128)(2,1)} %get-tuple-element.15.rope_ref, ...), custom_call_target="tpu_custom_call" | custom-call | flops 12000000000 | bytes 16000000 | tf_op jit(solution)/shard_map/attend/pallas_call | solution.py:552
  119.5 0.0 copy-start
  119.5 72.2 %give_back.1 = (bf16[256,4096]{1,0:T(8,128)(2,1)}, f32[16,4,128]{2,1,0:T(4,128)}) custom-call(bf16[2048,512]{1,0:T(8,128)(2,1)} %get-tuple-element.19.context_ref, f32[4,128]{1,0:T(4,128)} %get-tuple-element.20.peak_ref), custom_call_target="tpu_custom_call" | custom-call | tf_op jit(solution)/shard_map/give_back/pallas_call | solution.py:576
  191.8 0.8 slice_reduce_fusion
  192.6 0.1 reshape_squeeze.7
  192.7 0.1 broadcast_in_dim.8
  192.8 0.1 broadcast_bitcast_fusion
  192.9 0.1 broadcast_in_dim.7
  193.0 0.1 mul.20
  193.1 0.0 copy-done.2
  193.1 0.9 multiply_convert_fusion.1
  194.0 0.0 copy-done
  194.0 0.0 copy-start.1
  194.0 1.9 multiply_convert_fusion
  195.8 0.1 copy-done.1
  195.9 1.3 copy.15
  (3 shorter events, 0.0 us)
Async XLA Ops:
  82.7 110.3 %copy-start.2 = (bf16[64,4096]{1,0:T(8,128)(2,1)S(1)}, bf16[64,4096]{1,0:T(8,128)(2,1)}, u32[]{:S(2)}) copy-start(bf16[64,4096]{1,0:T(8,128)(2,1)} %uk_ref.1) | copy-start | bytes 1572868
  119.5 74.4 %copy-start = (bf16[192,6144]{1,0:T(8,128)(2,1)S(1)}, bf16[192,6144]{1,0:T(8,128)(2,1)}, u32[]{:S(2)}) copy-start(bf16[192,6144]{1,0:T(8,128)(2,1)} %uq_ref.1) | copy-start | bytes 7077892
  194.0 2.0 copy-start.1
where the time goes:
time: 197 us
  Pallas kernels  190 us (96%)
  local copies, waits for them, and re-layouts  4.16 us (2%)
  other arithmetic  2.79 us (1%)
    pallas_call x1, Pallas kernels, by_heads(): pl.pallas_call(functools.partial(spread, devices), out_shape=[jax.ShapeDt...  80.6 us
    pallas_call x1, Pallas kernels, by_heads(): pl.pallas_call(functools.partial(give_back, devices), out_shape=[jax.Shap...  72.2 us
    pallas_call x1, Pallas kernels, by_heads(): pl.pallas_call(functools.partial(attend, block, tile, own), out_shape=(ja...  36.8 us

commit v1 on v0

v1 whole, which is shorter than its diff:
```python
import functools
import math

import jax
import jax.numpy as jnp
import numpy as np
from jax import lax
from jax.experimental import pallas as pl
from jax.experimental.pallas import tpu as pltpu
from jax.sharding import PartitionSpec as P

NOPE = 128
ROPE = 64
VD = 128
CLIP = 8


rope_base = 50000.0
masked_value = -1e30


def turning(positions, width):
    steps = jnp.arange(width // 2, dtype=jnp.float32) * (2.0 / width)
    freqs = jnp.exp(-math.log(rope_base) * steps)
    angle = positions.astype(jnp.float32)[:, None] * freqs[None, :]
    return (jnp.cos(angle), jnp.sin(angle))


def rotate(values, cosine, sine):
    half = values.shape[-1] // 2
    first = values[..., :half]
    second = values[..., half:]
    return jnp.concatenate(
        [first * cosine - second * sine, second * cosine + first * sine], axis=-1
    )


def positions_of(index, order, half_block):
    which = index // half_block
    onehot = which[:, None] == jnp.arange(order.shape[0], dtype=jnp.int32)[None, :]
    base = jnp.sum(jnp.where(onehot, order[None, :], 0), axis=1)
    return base * half_block + index % half_block


def by_tokens(query_latent, key_latent, rope_key, w_uq, w_uk, w_uv, block_order, segment_ids):
    query_local, key_local = (
        lax.all_gather(query_latent[0], "tp", axis=1, tiled=True),
        lax.all_gather(key_latent[0], "tp", axis=1, tiled=True),
    )
    rows_uq, rows_uk, rows_uv = (
        lax.all_gather(w_uq, "seq", axis=0, tiled=True),
        lax.all_gather(w_uk, "seq", axis=0, tiled=True),
        lax.all_gather(w_uv, "seq", axis=0, tiled=True),
    )
    tok_rows = query_local.shape[0]
    half_block = tok_rows // 2
    order = block_order[0]
    labels_all = segment_ids[0]
    heads = w_uq.shape[1] // (NOPE + ROPE)
    scale = 1.0 / math.sqrt(NOPE + ROPE)
    own_index = lax.axis_index("seq") * tok_rows + jnp.arange(tok_rows, dtype=jnp.int32)
    query_pos = positions_of(own_index, order, half_block)
    query_labels = jnp.take(labels_all, query_pos)
    cosine, sine = turning(query_pos, ROPE)
    query_full = jnp.dot(query_local, rows_uq, preferred_element_type=jnp.float32).reshape(
        tok_rows, heads, NOPE + ROPE
    )
    query_nope = jnp.transpose(query_full[:, :, :NOPE].astype(jnp.bfloat16), (1, 0, 2))
    query_rope = jnp.transpose(
        rotate(query_full[:, :, NOPE:], cosine[:, None, :], sine[:, None, :]).astype(jnp.bfloat16),
        (1, 0, 2),
    )
    key_rope = rotate(rope_key[0].astype(jnp.float32), cosine, sine).astype(jnp.bfloat16)

    def slice_latent(pieces, first, width):
        latent_block = lax.dynamic_slice_in_dim(pieces[0], first, width, 0)
        rope_block = lax.dynamic_slice_in_dim(pieces[1], first, width, 0)
        nope_block = jnp.dot(latent_block, rows_uk, preferred_element_type=jnp.float32).astype(
            jnp.bfloat16
        )
        value_block = jnp.dot(latent_block, rows_uv, preferred_element_type=jnp.float32).astype(
            jnp.bfloat16
        )
        return (nope_block, value_block, rope_block)

    initial = (
        jnp.full((heads, tok_rows), masked_value, jnp.float32),
        jnp.zeros((heads, tok_rows), jnp.float32),
        jnp.zeros((heads, tok_rows, VD), jnp.float32),
    )
    pieces = (
        lax.all_gather(key_local, "seq", axis=0, tiled=True),
        lax.all_gather(key_rope, "seq", axis=0, tiled=True),
    )
    count = pieces[-1].shape[0]
    width = math.gcd(count, 512)

    def block_step(state, number):
        first = number * width
        nope_block, value_block, rope_block = slice_latent(pieces, first, width)
        nope_block = nope_block.reshape(width, heads, NOPE)
        value_block = value_block.reshape(width, heads, VD)
        key_index = first + jnp.arange(width, dtype=jnp.int32)
        key_pos = positions_of(key_index, order, half_block)
        key_labels = jnp.take(labels_all, key_pos)
        allowed = (key_pos[None, :] <= query_pos[:, None]) & (
            key_labels[None, :] == query_labels[:, None]
        )
        scores = jnp.einsum(
            "hqd,khd->hqk", query_nope, nope_block, preferred_element_type=jnp.float32
        )
        scores = (
            scores
            + jnp.einsum("hqr,kr->hqk", query_rope, rope_block, preferred_element_type=jnp.float32)
        ) * scale
        masked = jnp.where(allowed[None], scores, masked_value)
        run_max, run_total, run_sum = state
        new_max = jnp.maximum(run_max, jnp.max(masked, axis=2))
        weights = jnp.where(allowed[None], jnp.exp(masked - new_max[:, :, None]), 0.0)
        shrink = jnp.exp(run_max - new_max)
        new_total = run_total * shrink + jnp.sum(weights, axis=2)
        mixed = jnp.einsum(
            "hqk,khv->hqv",
            weights.astype(jnp.bfloat16),
            value_block,
            preferred_element_type=jnp.float32,
        )
        new_sum = run_sum * shrink[:, :, None] + mixed
        return ((new_max, new_total, new_sum), None)

    result, unused = lax.scan(block_step, initial, jnp.arange(count // width, dtype=jnp.int32))
    run_max, run_total, run_sum = result
    context = (run_sum / run_total[:, :, None]).astype(jnp.bfloat16)
    context = jnp.transpose(context, (1, 0, 2)).reshape(1, tok_rows, heads * VD)
    head_max = lax.pmax(jnp.max(run_max, axis=1), ("seq", "dp"))
    ratio = CLIP / jnp.maximum(head_max, CLIP)
    root = jnp.sqrt(ratio)
    factors = jnp.concatenate(
        [
            jnp.broadcast_to(root[:, None], (heads, NOPE)),
            jnp.broadcast_to(ratio[:, None], (heads, ROPE)),
        ],
        axis=1,
    ).reshape(heads * (NOPE + ROPE))
    clipped_uq = (w_uq.astype(jnp.float32) * factors[None, :]).astype(jnp.bfloat16)
    clipped_uk = (w_uk.astype(jnp.float32) * jnp.repeat(root, NOPE)[None, :]).astype(jnp.bfloat16)
    return (context, clipped_uq, clipped_uk)


def turned(values, cosine, sine):
    half = values.shape[-1] // 2
    swapped = jnp.concatenate([values[:, half:], values[:, :half]], axis=1)
    return values * cosine + swapped * sine


MESH = pl.DeviceIdType.MESH


def window(start, size):
    return pl.ds(pl.multiple_of(start * size, size), size)


def greet(wheres):
    barrier = pltpu.get_barrier_semaphore()
    for where in wheres:
        pl.semaphore_signal(barrier, inc=1, device_id=where, device_id_type=MESH)
    pl.semaphore_wait(barrier, len(wheres))


def fused(
    n, block, groups,
    order, inv_s, label_ref, query_ref, key_ref, rope_ref, uq_ref, uk_ref, uv_ref, turn_ref,
    out_ref, peaks_ref,
    q_lat, k_lat, r_lat, r_blk, wq_s, wk_s, wv_s, wvt_s, q_s, k_s, vt_s, s_s, p_s, c_s, lab_s, turn_s,
    peak_s,
    got_q, got_k, got_r, got_w, got_c, got_p,
    sent_l, sent_w, sent_x, sent_m, sent_c, sent_p, local_l, local_w, local_c,
):
    s, t, d = lax.axis_index("seq"), lax.axis_index("tp"), lax.axis_index("dp")
    quarter = n // 2
    level, core = s // 2, lax.rem(s, 2)
    half = s // quarter
    place = lax.rem(s, quarter)
    first_of_half = half * quarter
    mate = s + 1 - 2 * core
    pair = first_of_half + lax.rem(place + 2, quarter)
    inner = (level == quarter // 2 - 1) | (level == quarter // 2)
    gate = jnp.where(half == 0, quarter, quarter - 2) + core
    far = [(1 - half) * quarter + 2 * k + core for k in range(2)]
    others = [lax.rem(s + k, n) for k in range(1, n)]
    to_mate, to_pair, to_gate = {"seq": mate}, {"seq": pair}, {"seq": gate}
    beside, across = {"tp": 1 - t}, {"dp": 1 - d}
    peers = [{"seq": to} for to in others] + [across] + [{"seq": to, "dp": 1 - d} for to in others]
    greet(peers + [beside])

    rows, wide = query_ref.shape
    part, unused, thin = key_ref.shape
    blocks = k_lat.shape[0]
    count = blocks * block
    own_blocks = blocks // 2
    back = blocks // 2
    scale = 1.0 / math.sqrt(NOPE + ROPE)
    turn_width = NOPE + ROPE

    def link(source, target, arrived, where, sender):
        return pltpu.make_async_remote_copy(
            src_ref=source, dst_ref=target, send_sem=sender, recv_sem=arrived,
            device_id=where, device_id_type=MESH,
        )

    def arrive(target, arrived):
        link(target, target, arrived, beside, sent_l.at[0]).wait_recv()

    started = []

    def send(source, spot, where, condition=None):
        target, arrived = spot
        copy = link(source, target, arrived, where, sent_l.at[len(started)])
        if condition is None:
            copy.start()
        else:
            pl.when(condition)(copy.start)
        started.append((copy, condition))

    def q_spot(src, tp):
        at = lax.rem(src, quarter)
        return (q_lat.at[window(at, rows), window(tp, wide)], got_q.at[at, tp])

    def k_spot(src, tp):
        return (k_lat.at[window(src, part), :, window(tp, thin)], got_k.at[src, tp])

    def r_spot(src):
        return (r_lat.at[:, window(src, rows)], got_r.at[src])

    for where in (to_gate, to_pair):
        send(key_ref, k_spot(s, t), where)
        send(rope_ref, r_spot(s), where)
    send(query_ref, q_spot(s, t), to_pair)
    send(key_ref, k_spot(s, t), beside)
    send(query_ref, q_spot(s, t), beside)
    send(key_ref, k_spot(s, t), to_mate)
    send(rope_ref, r_spot(s), to_mate)
    send(query_ref, q_spot(s, t), to_mate)

    weights = ((uq_ref, wq_s), (uk_ref, wk_s), (uv_ref, wv_s))

    def w_spot(g, index, src):
        ref, held = weights[index]
        return (held.at[g, window(src, ref.shape[0]), :], got_w.at[g, index, src])

    def w_piece(g, index, to):
        ref, held = weights[index]
        return ref.at[:, window(lax.rem(to, quarter) * groups + g, held.shape[2])]

    def w_copy(g, index, slot, to):
        target, arrived = w_spot(g, index, s)
        return link(w_piece(g, index, to), target, arrived, {"seq": to}, sent_w.at[g, index, slot])

    far_to = [(1 - half) * quarter + k for k in range(quarter)]
    pair_chip = pair - core
    near_to = [pair_chip, pair_chip + 1]
    sender = core == d

    def far_copies(g):
        return [w_copy(g, i, k, to) for k, to in enumerate(far_to) for i in range(3)]

    def near_copies(g):
        return [w_copy(g, i, quarter + k, to) for k, to in enumerate(near_to) for i in range(3)]

    def start_all(copies):
        for copy in copies:
            copy.start()

    def first_weights(g, unused):
        start_all(far_copies(g))
        pl.when((g == 0) | ~inner)(lambda: start_all(near_copies(g)))
        return unused

    @pl.when(sender)
    def _():
        lax.fori_loop(0, groups, first_weights, 0)


    def mate_copies(g):
        out = []
        for i in range(3):
            target, arrived = w_spot(g, i, s)
            out.append(link(w_piece(g, i, mate), target, arrived, to_mate, sent_m.at[g, i]))
        return out

    def kept_weights(g):
        return [
            pltpu.make_async_copy(w_piece(g, i, s), w_spot(g, i, s)[0], local_w.at[g, i])
            for i in range(3)
        ]

    def near_weights(g, unused):
        start_all(kept_weights(g))
        start_all(mate_copies(g))
        return unused

    lax.fori_loop(0, groups, near_weights, 0)

    kept = [
        pltpu.make_async_copy(key_ref, k_spot(s, t)[0], local_l.at[0]),
        pltpu.make_async_copy(rope_ref, r_spot(s)[0], local_l.at[1]),
        pltpu.make_async_copy(query_ref, q_spot(s, t)[0], local_l.at[2]),
        pltpu.make_async_copy(turn_ref, turn_s, local_l.at[3]),
    ]
    start_all(kept)

    def label_step(p, unused):
        lab_s[back + p] = jnp.transpose(jnp.broadcast_to(label_ref[p], (block, block)))
        return unused

    lax.fori_loop(0, blocks, label_step, 0)

    def empty_step(p, unused):
        lab_s[p] = jnp.full((block, block), -1, jnp.int32)
        for head in range(2):
            k_s[head, p] = jnp.zeros((block, turn_width), jnp.bfloat16)
        vt_s[p] = jnp.zeros((2 * VD, block), jnp.bfloat16)
        return unused

    lax.fori_loop(0, back, empty_step, 0)

    def pass_keys(src, onward):
        arrive(*k_spot(src, t))
        arrive(*r_spot(src))
        if onward:
            send(k_spot(src, t)[0], k_spot(src, t), to_pair, inner)
            send(r_spot(src)[0], r_spot(src), to_pair, inner)
        send(k_spot(src, t)[0], k_spot(src, t), beside)
        send(k_spot(src, t)[0], k_spot(src, t), to_mate)
        send(r_spot(src)[0], r_spot(src), to_mate)

    def hand_keys(src):
        arrive(*k_spot(src, 1 - t))
        send(k_spot(src, 1 - t)[0], k_spot(src, 1 - t), to_mate)

    def hand_query(src):
        arrive(*q_spot(src, 1 - t))
        send(q_spot(src, 1 - t)[0], q_spot(src, 1 - t), to_mate)

    pass_keys(pair, False)
    for src in far:
        pass_keys(src, True)

    def later_weights(g, unused):
        start_all(near_copies(g))
        return unused

    @pl.when(sender & inner)
    def _():
        lax.fori_loop(1, groups, later_weights, 0)

    arrive(*q_spot(pair, t))
    send(q_spot(pair, t)[0], q_spot(pair, t), beside)
    send(q_spot(pair, t)[0], q_spot(pair, t), to_mate)
    hand_keys(s)
    hand_query(s)
    hand_keys(pair)
    for src in far:
        hand_keys(src)
    hand_query(pair)

    across_from = [lax.rem(level + k, quarter) * 2 for k in range(1, quarter)]

    def forward(g, k):
        src = across_from[k] + d
        for i in range(3):
            target, arrived = w_spot(g, i, src)
            arrive(target, arrived)
            link(target, target, arrived, across, sent_x.at[g, i, k]).start()

    for k in range(len(across_from)):
        forward(0, k)

    parity = 1 - core
    for src in (mate, pair + 1 - 2 * core):
        arrive(*q_spot(src, t))
        arrive(*q_spot(src, 1 - t))
    for k in range(quarter):
        src = 2 * k + parity
        arrive(*k_spot(src, t))
        arrive(*k_spot(src, 1 - t))
        arrive(*r_spot(src))
    for copy in kept:
        copy.wait()

    for b in range(blocks):
        r_blk[b] = r_lat[:, b * block : (b + 1) * block]

    def rope_step(p, unused):
        raw = jnp.transpose(r_blk[inv_s[p]].astype(jnp.float32))
        turned_key = turned(raw, turn_s[p, :, :ROPE], turn_s[p, :, ROPE:]).astype(jnp.bfloat16)
        for head in range(2):
            k_s[head, p + back, :, NOPE:] = turned_key
        return unused

    lax.fori_loop(0, blocks, rope_step, 0)

    step_blocks = 4
    chunk = step_blocks * block
    factor = scale * math.log2(math.e)

    def out_spot(g, src):
        at = lax.rem(src, quarter)
        return (out_ref.at[:, window(at * groups + g, 2 * VD)], got_c.at[g, at])

    def context_copies(g):
        out = []
        for k in range(1, quarter):
            at = lax.rem(place + k, quarter)
            target, arrived = out_spot(g, s)
            out.append(
                link(
                    c_s.at[g, window(at, rows), :], target, arrived,
                    {"seq": first_of_half + at}, sent_c.at[g, k - 1],
                )
            )
        return out

    def kept_context(g):
        return pltpu.make_async_copy(
            c_s.at[g, window(place, rows), :], out_spot(g, s)[0], local_c.at[g]
        )

    def group(g, unused):
        for k in range(len(across_from)):
            for i in range(3):
                arrive(*w_spot(g, i, across_from[k] + 1 - d))
        for i in range(3):
            arrive(*w_spot(g, i, mate))
        for copy in kept_weights(g):
            copy.wait()

        wvt_s[...] = jnp.transpose(wv_s[g])

        def keys(step, unused):
            latent = jnp.concatenate(
                [k_lat[inv_s[step * step_blocks + j]] for j in range(step_blocks)], axis=0
            )
            nope = jnp.dot(latent, wk_s[g], preferred_element_type=jnp.float32)
            nope = nope.astype(jnp.bfloat16)
            value = lax.dot_general(
                wvt_s[...], latent, (((1,), (1,)), ((), ())), preferred_element_type=jnp.float32
            )
            value = value.astype(jnp.bfloat16)
            for j in range(step_blocks):
                at, lo, hi = back + step * step_blocks + j, j * block, (j + 1) * block
                for head in range(2):
                    k_s[head, at, :, :NOPE] = nope[lo:hi, head * NOPE : (head + 1) * NOPE]
                vt_s[at] = value[:, lo:hi]
            return unused

        lax.fori_loop(0, blocks // step_blocks, keys, 0)

        def queries(step, unused):
            full = jnp.dot(
                q_lat[window(step, chunk), :], wq_s[g], preferred_element_type=jnp.float32
            )
            for j in range(step_blocks):
                b = step * step_blocks + j
                turns = turn_s[order[half * own_blocks + b]]
                cosine, sine = turns[:, :ROPE], turns[:, ROPE:]
                lo, hi = j * block, (j + 1) * block
                here = window(b, block)
                for head in range(2):
                    base = head * turn_width
                    q_s[head, here, :NOPE] = full[lo:hi, base : base + NOPE].astype(jnp.bfloat16)
                    q_s[head, here, NOPE:] = turned(
                        full[lo:hi, base + NOPE : base + turn_width], cosine, sine
                    ).astype(jnp.bfloat16)
            return unused

        lax.fori_loop(0, own_blocks // step_blocks, queries, 0)

        def attend(b, best):
            for k in range(len(across_from)):
                pl.when((b == 2 * k) & (g + 1 < groups))(lambda k=k: forward(g + 1, k))
            p = order[half * own_blocks + b]
            here = window(b, block)
            asking = label_ref[p]
            causal = lax.broadcasted_iota(jnp.int32, (block, block), 0) <= (
                lax.broadcasted_iota(jnp.int32, (block, block), 1)
            )
            raws = [
                lax.dot_general(
                    jnp.concatenate([k_s[head, p + j] for j in range(back + 1)], axis=0),
                    q_s[head, here, :], (((1,), (1,)), ((), ())),
                    preferred_element_type=jnp.float32,
                )
                for head in range(2)
            ]
            tops = [jnp.full((8, block), masked_value, jnp.float32) for head in range(2)]
            for j in range(back + 1):
                lo, hi = j * block, (j + 1) * block
                allowed = lab_s[p + j] == asking
                if j == back:
                    allowed = allowed & causal
                for head in range(2):
                    raw = jnp.where(allowed, raws[head][lo:hi, :], masked_value)
                    s_s[head, lo:hi, :] = raw
                    tops[head] = jnp.maximum(
                        tops[head], jnp.max(raw.reshape(block // 8, 8, block), axis=0)
                    )
            out = []
            for head in range(2):
                top = jnp.max(tops[head], axis=0, keepdims=True)
                total = jnp.zeros((8, block), jnp.float32)
                for j in range(back + 1):
                    lo, hi = j * block, (j + 1) * block
                    piece = jnp.exp2((s_s[head, lo:hi, :] - top) * factor)
                    total = total + jnp.sum(piece.reshape(block // 8, 8, block), axis=0)
                    p_s[head, lo:hi, :] = piece.astype(jnp.bfloat16)
                mixed = jnp.dot(
                    jnp.concatenate(
                        [vt_s[p + j, head * VD : (head + 1) * VD, :] for j in range(back + 1)], axis=1
                    ),
                    p_s[head],
                    preferred_element_type=jnp.float32,
                )
                done = mixed / jnp.sum(total, axis=0, keepdims=True)
                c_s[g, here, head * VD : (head + 1) * VD] = jnp.transpose(done).astype(
                    jnp.bfloat16
                )
                out.append(jnp.maximum(best[head], top))
            return tuple(out)

        low = jnp.full((1, block), masked_value, jnp.float32)
        best = lax.fori_loop(0, own_blocks, attend, (low, low))
        peak_s[g] = jnp.concatenate(best, axis=0) * scale
        start_all(context_copies(g))
        kept_context(g).start()
        return unused

    lax.fori_loop(0, groups, group, 0)

    me = d * n + s
    peak_copies = [
        link(peak_s, peaks_ref.at[me], got_p.at[me], where, sent_p.at[k])
        for k, where in enumerate(peers)
    ]
    start_all(peak_copies)
    keep_peak = pltpu.make_async_copy(peak_s, peaks_ref.at[me], local_l.at[4])
    keep_peak.start()

    def settle(g, unused):
        def far_sent():
            for copy in far_copies(g) + near_copies(g):
                copy.wait_send()

        pl.when(sender)(far_sent)
        for copy in mate_copies(g):
            copy.wait_send()
        for k in range(len(across_from)):
            for i in range(3):
                target, arrived = w_spot(g, i, across_from[k] + d)
                link(target, target, arrived, across, sent_x.at[g, i, k]).wait_send()
        for copy in context_copies(g):
            copy.wait_send()
        kept_context(g).wait()
        for k in range(1, quarter):
            arrive(*out_spot(g, first_of_half + lax.rem(place + k, quarter)))
        return unused

    lax.fori_loop(0, groups, settle, 0)
    for copy, condition in started:
        if condition is None:
            copy.wait_send()
        else:
            pl.when(condition)(copy.wait_send)
    for copy in peak_copies:
        copy.wait_send()
    keep_peak.wait()
    for src in [d * n + to for to in others] + [(1 - d) * n + to for to in others] + [(1 - d) * n + s]:
        arrive(peaks_ref.at[src], got_p.at[src])


def by_halves(query_latent, key_latent, rope_key, w_uq, w_uk, w_uv, block_order, segment_ids):
    devices = lax.axis_size("seq")
    sides = lax.axis_size("tp")
    heads = w_uq.shape[1] // (NOPE + ROPE)
    quarter = devices // 2
    groups = heads // quarter // 2
    rows = query_latent.shape[1]
    order, labels = block_order[0], segment_ids[0]
    count, blocks = labels.shape[0], order.shape[0]
    block = count // blocks
    back = blocks // 2
    anyplace = pl.BlockSpec(memory_space=pl.ANY)
    vmem = pl.BlockSpec(memory_space=pltpu.VMEM)
    smem = pl.BlockSpec(memory_space=pltpu.SMEM)
    steps = np.arange(ROPE // 2, dtype=np.float32) * np.float32(2.0 / ROPE)
    freqs = np.exp(np.float32(-math.log(rope_base)) * steps).astype(np.float32)
    angle = np.arange(count, dtype=np.float32)[:, None] * freqs[None, :]
    cosine, sine = np.cos(angle), np.sin(angle)
    turns = jnp.asarray(np.concatenate([cosine, cosine, -sine, sine], axis=1), jnp.float32)
    every = jnp.arange(blocks, dtype=jnp.int32)
    stored_at = jnp.sum(jnp.where(order[None, :] == every[:, None], every[None, :], 0), axis=1)
    bf, f32 = jnp.bfloat16, jnp.float32
    dma = pltpu.SemaphoreType.DMA
    context, peaks = pl.pallas_call(
        functools.partial(fused, devices, block, groups),
        out_shape=[
            jax.ShapeDtypeStruct((rows, heads * VD), bf),
            jax.ShapeDtypeStruct((2 * devices, groups, 2, block), f32),
        ],
        in_specs=[smem, smem, vmem] + [anyplace] * 7,
        out_specs=[anyplace, vmem],
        scratch_shapes=[
            pltpu.VMEM((count // 2, sides * query_latent.shape[2]), bf),
            pltpu.VMEM((blocks, block, sides * key_latent.shape[2]), bf),
            pltpu.VMEM((ROPE, count), bf),
            pltpu.VMEM((blocks, ROPE, block), bf),
            pltpu.VMEM((groups, devices * w_uq.shape[0], 2 * (NOPE + ROPE)), bf),
            pltpu.VMEM((groups, devices * w_uk.shape[0], 2 * NOPE), bf),
            pltpu.VMEM((groups, devices * w_uv.shape[0], 2 * VD), bf),
            pltpu.VMEM((2 * VD, devices * w_uv.shape[0]), bf),
            pltpu.VMEM((2, count // 2, NOPE + ROPE), bf),
            pltpu.VMEM((2, back + blocks, block, NOPE + ROPE), bf),
            pltpu.VMEM((back + blocks, 2 * VD, block), bf),
            pltpu.VMEM((2, (back + 1) * block, block), f32),
            pltpu.VMEM((2, (back + 1) * block, block), bf),
            pltpu.VMEM((groups, count // 2, 2 * VD), bf),
            pltpu.VMEM((back + blocks, block, block), jnp.int32),
            pltpu.VMEM((blocks, block, 2 * ROPE), f32),
            pltpu.VMEM((groups, 2, block), f32),
            dma((quarter, sides)),
            dma((devices, sides)),
            dma((devices,)),
            dma((groups, 3, devices)),
            dma((groups, quarter)),
            dma((2 * devices,)),
            dma((40,)),
            dma((groups, 3, quarter + 2)),
            dma((groups, 3, quarter - 1)),
            dma((groups, 3)),
            dma((groups, quarter - 1)),
            dma((2 * devices,)),
            dma((5,)),
            dma((groups, 3)),
            dma((groups,)),
        ],
        compiler_params=pltpu.CompilerParams(
            collective_id=0, has_side_effects=True, vmem_limit_bytes=60 * 1024 * 1024
        ),
        name="fused",
    )(
        order, stored_at, labels.reshape(blocks, 1, block), query_latent[0],
        key_latent[0].reshape(rows // block, block, key_latent.shape[2]),
        jnp.transpose(rope_key[0]), w_uq, w_uk, w_uv, turns.reshape(blocks, block, 2 * ROPE),
    )
    head_max = jnp.max(peaks.reshape(2, 2, heads, block), axis=(0, 1, 3))
    return (context[None],) + clipped(w_uq, w_uk, head_max, heads)


def clipped(w_uq, w_uk, head_max, heads):
    ratio = CLIP / jnp.maximum(head_max, CLIP)
    root = jnp.sqrt(ratio)
    factors = jnp.concatenate(
        [
            jnp.broadcast_to(root[:, None], (heads, NOPE)),
            jnp.broadcast_to(ratio[:, None], (heads, ROPE)),
        ],
        axis=1,
    ).reshape(heads * (NOPE + ROPE))
    clipped_uq = (w_uq.astype(jnp.float32) * factors[None, :]).astype(jnp.bfloat16)
    clipped_uk = (w_uk.astype(jnp.float32) * jnp.repeat(root, NOPE)[None, :]).astype(jnp.bfloat16)
    return (clipped_uq, clipped_uk)


def on_device(*arrays):
    heads = arrays[3].shape[1] // (NOPE + ROPE)
    pairs = lax.axis_size("tp") == 2 and lax.axis_size("dp") == 2
    if pairs and lax.axis_size("seq") == 8 and heads % 8 == 0:
        return by_halves(*arrays)
    return by_tokens(*arrays)


def solution(mesh):
    placed = (
        P("dp", "seq", "tp"),
        P("dp", "seq", "tp"),
        P("dp", "seq", None),
        P("seq", "tp"),
        P("seq", "tp"),
        P("seq", "tp"),
        P("dp", None),
        P("dp", None),
    )
    return jax.shard_map(
        on_device,
        mesh=mesh,
        in_specs=placed,
        out_specs=(P("dp", "seq", "tp"), P("seq", "tp"), P("seq", "tp")),
        check_vma=False,
    )
```

time: 197 us -> 164 us (0.83)
  Pallas kernels: 190 us -> 156 us
  local copies, waits for them, and re-layouts: 4.16 us -> 1.73 us
  other arithmetic: 2.79 us -> 5.07 us
    pallas_call x3 -> x1, Pallas kernels: 190 us -> 156 us  [by_halves(): pl.pallas_call(functools.partial(fused, devices, block, groups), out_shap...]
where the time goes in v1:
time: 164 us
  Pallas kernels  156 us (95%)
  other arithmetic  5.07 us (3%)
  local copies, waits for them, and re-layouts  1.73 us (1%)
    pallas_call x1, Pallas kernels, by_halves(): pl.pallas_call(functools.partial(fused, devices, block, groups), out_shap...  156 us

profile of v1, /device:TPU:13, one launch (start us, length us, event | category | flops | bytes accessed | tf_op | source)
XLA Modules:
  0.0 163.6 jit_solution(10244674763078522554)
XLA Ops:
  0.6 1.3 select_reduce_fusion.inv_s
  1.9 0.0 copy-start
  1.9 156.2 %fused.1 = (bf16[256,4096]{1,0:T(8,128)(2,1)}, f32[16,4,2,128]{3,2,1,0:T(2,128)}) custom-call(s32[16]{0:T(128)} %bitcast.16, s32[16]{0:T(128)} %select_reduce_fusion.inv_s, s32[16,1,128]{2,1,0:T(1,128)} %bitcast.14, bf16[256,768]{1,0:T(8,128)(2,1)} %bitcast.11, bf16[2,128,256]{2,1,0:T(8,128)(2,1)} %bitcast.12, bf16[64,256]{1,0:T(8,128)(2,1)} %bitcast.13, ...), custom_call_target="tpu_custom_call" | custom-call | tf_op jit(solution)/shard_map/fused/pallas_call | solution.py:604
  158.1 1.0 reduce_max.10
  159.1 0.1 reduce_max.14
  159.2 0.1 broadcast_in_dim.34
  159.3 0.1 broadcast_in_dim.33
  159.4 0.1 mul.20
  159.5 0.0 copy-done
  159.5 0.0 copy-start.2
  159.5 0.0 copy-start.1
  159.5 1.9 %multiply_convert_fusion = bf16[192,6144]{1,0:T(8,128)(2,1)} fusion(bf16[192,6144]{1,0:T(8,128)(2,1)S(1)} %copy-done, f32[6144]{0:T(1024)S(1)} %mul.20), kind=kLoop, calls=%fused_computation | loop fusion | flops 3538944 | bytes 4743168 | tf_op jit(solution)/shard_map/convert_element_type | solution.py:669
  161.4 0.1 broadcast_bitcast_fusion
  161.4 0.0 copy-done.2
  161.4 0.9 multiply_convert_fusion.1
  162.3 0.0 copy-done.1
  162.3 1.3 copy.13
  (3 shorter events, 0.0 us)
Async XLA Ops:
  1.9 157.5 %copy-start = (bf16[192,6144]{1,0:T(8,128)(2,1)S(1)}, bf16[192,6144]{1,0:T(8,128)(2,1)}, u32[]{:S(2)}) copy-start(bf16[192,6144]{1,0:T(8,128)(2,1)} %uq_ref.1) | copy-start | bytes 7077892
  159.5 2.0 %copy-start.2 = (bf16[64,4096]{1,0:T(8,128)(2,1)S(1)}, bf16[64,4096]{1,0:T(8,128)(2,1)}, u32[]{:S(2)}) copy-start(bf16[64,4096]{1,0:T(8,128)(2,1)} %uk_ref.1) | copy-start | bytes 1572868
  159.5 2.8 %copy-start.1 = (bf16[256,4096]{1,0:T(8,128)(2,1)S(1)}, bf16[256,4096]{1,0:T(8,128)(2,1)}, u32[]{:S(2)}) copy-start(bf16[256,4096]{1,0:T(8,128)(2,1)} %get-tuple-element.5) | copy-start | bytes 6291460

commit v2 on v1

--- a/solution.py
+++ b/solution.py
@@ -169,10 +169,10 @@
 
 def fused(
     n, block, groups,
-    order, inv_s, label_ref, query_ref, key_ref, rope_ref, uq_ref, uk_ref, uv_ref, turn_ref,
+    order, label_ref, query_ref, key_ref, rope_ref, uq_ref, uk_ref, uv_ref, turn_ref,
     out_ref, peaks_ref,
     q_lat, k_lat, r_lat, r_blk, wq_s, wk_s, wv_s, wvt_s, q_s, k_s, vt_s, s_s, p_s, c_s, lab_s, turn_s,
-    peak_s,
+    peak_s, inv_s,
     got_q, got_k, got_r, got_w, got_c, got_p,
     sent_l, sent_w, sent_x, sent_m, sent_c, sent_p, local_l, local_w, local_c,
 ):
@@ -212,15 +212,18 @@
         link(target, target, arrived, beside, sent_l.at[0]).wait_recv()
 
     started = []
-
-    def send(source, spot, where, condition=None):
-        target, arrived = spot
-        copy = link(source, target, arrived, where, sent_l.at[len(started)])
-        if condition is None:
-            copy.start()
-        else:
-            pl.when(condition)(copy.start)
-        started.append((copy, condition))
+    state = {"when": None}
+
+    def send(source, spot, where):
+        target, arrived = spot()
+        source = target if source is None else source
+        link(source, target, arrived, where, sent_l.at[len(started)]).start()
+        started.append((spot, where, state["when"]))
+
+    def under(condition, action):
+        state["when"] = condition
+        pl.when(condition)(action)
+        state["when"] = None
 
     def q_spot(src, tp):
         at = lax.rem(src, quarter)
@@ -233,16 +236,16 @@
         return (r_lat.at[:, window(src, rows)], got_r.at[src])
 
     for where in (to_gate, to_pair):
-        send(key_ref, k_spot(s, t), where)
-        send(rope_ref, r_spot(s), where)
-    send(query_ref, q_spot(s, t), to_pair)
-    send(key_ref, k_spot(s, t), beside)
-    send(query_ref, q_spot(s, t), beside)
-    send(key_ref, k_spot(s, t), to_mate)
-    send(rope_ref, r_spot(s), to_mate)
-    send(query_ref, q_spot(s, t), to_mate)
-
-    weights = ((uq_ref, wq_s), (uk_ref, wk_s), (uv_ref, wv_s))
+        send(key_ref, lambda: k_spot(s, t), where)
+        send(rope_ref, lambda: r_spot(s), where)
+    send(query_ref, lambda: q_spot(s, t), to_pair)
+    send(key_ref, lambda: k_spot(s, t), beside)
+    send(query_ref, lambda: q_spot(s, t), beside)
+    send(key_ref, lambda: k_spot(s, t), to_mate)
+    send(rope_ref, lambda: r_spot(s), to_mate)
+    send(query_ref, lambda: q_spot(s, t), to_mate)
+
+    weights = ((uk_ref, wk_s), (uv_ref, wv_s), (uq_ref, wq_s))
 
     def w_spot(g, index, src):
         ref, held = weights[index]
@@ -256,7 +259,9 @@
         target, arrived = w_spot(g, index, s)
         return link(w_piece(g, index, to), target, arrived, {"seq": to}, sent_w.at[g, index, slot])
 
-    far_to = [(1 - half) * quarter + k for k in range(quarter)]
+    far_to = [
+        (1 - half) * quarter + lax.rem(k + 2 * lax.rem(level, 2), quarter) for k in range(quarter)
+    ]
     pair_chip = pair - core
     near_to = [pair_chip, pair_chip + 1]
     sender = core == d
@@ -271,14 +276,11 @@
         for copy in copies:
             copy.start()
 
-    def first_weights(g, unused):
-        start_all(far_copies(g))
-        pl.when((g == 0) | ~inner)(lambda: start_all(near_copies(g)))
-        return unused
-
-    @pl.when(sender)
-    def _():
-        lax.fori_loop(0, groups, first_weights, 0)
+    def send_weights(g):
+        start_all(near_copies(g) + far_copies(g))
+
+    pl.when(sender & ~inner)(lambda: start_all(near_copies(0)))
+    pl.when(sender)(lambda: start_all(far_copies(0)))
 
 
     def mate_copies(g):
@@ -310,6 +312,10 @@
     start_all(kept)
 
     def label_step(p, unused):
+        at = 0
+        for b in range(blocks):
+            at = jnp.where(order[b] == p, b, at)
+        inv_s[p] = at
         lab_s[back + p] = jnp.transpose(jnp.broadcast_to(label_ref[p], (block, block)))
         return unused
 
@@ -328,43 +334,34 @@
         arrive(*k_spot(src, t))
         arrive(*r_spot(src))
         if onward:
-            send(k_spot(src, t)[0], k_spot(src, t), to_pair, inner)
-            send(r_spot(src)[0], r_spot(src), to_pair, inner)
-        send(k_spot(src, t)[0], k_spot(src, t), beside)
-        send(k_spot(src, t)[0], k_spot(src, t), to_mate)
-        send(r_spot(src)[0], r_spot(src), to_mate)
+            send(None, lambda: k_spot(src, t), to_pair)
+            send(None, lambda: r_spot(src), to_pair)
+        send(None, lambda: k_spot(src, t), beside)
+        send(None, lambda: k_spot(src, t), to_mate)
+        send(None, lambda: r_spot(src), to_mate)
 
     def hand_keys(src):
         arrive(*k_spot(src, 1 - t))
-        send(k_spot(src, 1 - t)[0], k_spot(src, 1 - t), to_mate)
+        send(None, lambda: k_spot(src, 1 - t), to_mate)
 
     def hand_query(src):
         arrive(*q_spot(src, 1 - t))
-        send(q_spot(src, 1 - t)[0], q_spot(src, 1 - t), to_mate)
-
-    pass_keys(pair, False)
-    for src in far:
-        pass_keys(src, True)
-
-    def later_weights(g, unused):
-        start_all(near_copies(g))
-        return unused
-
-    @pl.when(sender & inner)
-    def _():
-        lax.fori_loop(1, groups, later_weights, 0)
-
-    arrive(*q_spot(pair, t))
-    send(q_spot(pair, t)[0], q_spot(pair, t), beside)
-    send(q_spot(pair, t)[0], q_spot(pair, t), to_mate)
-    hand_keys(s)
-    hand_query(s)
-    hand_keys(pair)
-    for src in far:
-        hand_keys(src)
-    hand_query(pair)
-
-    across_from = [lax.rem(level + k, quarter) * 2 for k in range(1, quarter)]
+        send(None, lambda: q_spot(src, 1 - t), to_mate)
+
+    def turn_ropes():
+        for b in range(blocks):
+            r_blk[b] = r_lat[:, b * block : (b + 1) * block]
+
+        def rope_step(p, unused):
+            raw = jnp.transpose(r_blk[inv_s[p]].astype(jnp.float32))
+            turned_key = turned(raw, turn_s[p, :, :ROPE], turn_s[p, :, ROPE:]).astype(jnp.bfloat16)
+            for head in range(2):
+                k_s[head, p + back, :, NOPE:] = turned_key
+            return unused
+
+        lax.fori_loop(0, blocks, rope_step, 0)
+
+    across_from = [pair_chip, gate - core, 2 * (1 - half) * quarter + quarter - 2 - (gate - core)]
 
     def forward(g, k):
         src = across_from[k] + d
@@ -373,32 +370,47 @@
             arrive(target, arrived)
             link(target, target, arrived, across, sent_x.at[g, i, k]).start()
 
-    for k in range(len(across_from)):
-        forward(0, k)
-
-    parity = 1 - core
-    for src in (mate, pair + 1 - 2 * core):
-        arrive(*q_spot(src, t))
-        arrive(*q_spot(src, 1 - t))
+    def pass_query():
+        arrive(*q_spot(pair, t))
+        send(None, lambda: q_spot(pair, t), beside)
+        send(None, lambda: q_spot(pair, t), to_mate)
+
+    def relay():
+        for src in far:
+            pass_keys(src, True)
+
+    def take():
+        for src in far:
+            pass_keys(src, False)
+
+    pass_keys(pair, False)
+    under(inner, relay)
+    pl.when(sender & inner)(lambda: start_all(near_copies(0)))
+    hand_keys(s)
+    hand_query(s)
+    pass_query()
+    hand_keys(pair)
+    forward(0, 1)
+    pl.when(sender)(lambda: send_weights(1))
+    forward(0, 2)
+    under(~inner, take)
+    for src in far:
+        hand_keys(src)
+    hand_query(pair)
+    forward(0, 0)
+    pl.when(sender)(lambda: send_weights(2))
+
     for k in range(quarter):
-        src = 2 * k + parity
+        src = 2 * k + 1 - core
         arrive(*k_spot(src, t))
         arrive(*k_spot(src, 1 - t))
         arrive(*r_spot(src))
     for copy in kept:
         copy.wait()
-
-    for b in range(blocks):
-        r_blk[b] = r_lat[:, b * block : (b + 1) * block]
-
-    def rope_step(p, unused):
-        raw = jnp.transpose(r_blk[inv_s[p]].astype(jnp.float32))
-        turned_key = turned(raw, turn_s[p, :, :ROPE], turn_s[p, :, ROPE:]).astype(jnp.bfloat16)
-        for head in range(2):
-            k_s[head, p + back, :, NOPE:] = turned_key
-        return unused
-
-    lax.fori_loop(0, blocks, rope_step, 0)
+    turn_ropes()
+    for src in (mate, pair + 1 - 2 * core):
+        arrive(*q_spot(src, t))
+        arrive(*q_spot(src, 1 - t))
 
     step_blocks = 4
     chunk = step_blocks * block
@@ -408,25 +420,37 @@
         at = lax.rem(src, quarter)
         return (out_ref.at[:, window(at * groups + g, 2 * VD)], got_c.at[g, at])
 
-    def context_copies(g):
-        out = []
-        for k in range(1, quarter):
-            at = lax.rem(place + k, quarter)
-            target, arrived = out_spot(g, s)
-            out.append(
-                link(
-                    c_s.at[g, window(at, rows), :], target, arrived,
-                    {"seq": first_of_half + at}, sent_c.at[g, k - 1],
-                )
-            )
-        return out
+    other_chip = lax.rem(place - core + 2, quarter)
+
+    def context_to(g, k):
+        at = lax.rem(other_chip + k, quarter)
+        target, arrived = out_spot(g, s)
+        return link(
+            c_s.at[g, window(at, rows), :], target, arrived,
+            {"seq": first_of_half + at}, sent_c.at[g, k],
+        )
 
     def kept_context(g):
         return pltpu.make_async_copy(
             c_s.at[g, window(place, rows), :], out_spot(g, s)[0], local_c.at[g]
         )
 
+    def leave(g, k):
+        if k < 2:
+            context_to(g, k).start()
+        else:
+            pl.when(core == k - 2)(kept_context(g).start)
+            pl.when(core != k - 2)(context_to(g, k).start)
+
+    def left(g):
+        for k in range(2):
+            context_to(g, k).wait_send()
+        for k in range(2, 4):
+            pl.when(core != k - 2)(context_to(g, k).wait_send)
+        kept_context(g).wait()
+
     def group(g, unused):
+        pl.when(sender & (g + 3 < groups))(lambda: send_weights(g + 3))
         for k in range(len(across_from)):
             for i in range(3):
                 arrive(*w_spot(g, i, across_from[k] + 1 - d))
@@ -434,6 +458,9 @@
             arrive(*w_spot(g, i, mate))
         for copy in kept_weights(g):
             copy.wait()
+
+        def onward(k):
+            pl.when(g + 1 < groups)(lambda: forward(g + 1, k))
 
         wvt_s[...] = jnp.transpose(wv_s[g])
 
@@ -454,7 +481,9 @@
                 vt_s[at] = value[:, lo:hi]
             return unused
 
+        onward(0)
         lax.fori_loop(0, blocks // step_blocks, keys, 0)
+        onward(1)
 
         def queries(step, unused):
             full = jnp.dot(
@@ -475,10 +504,10 @@
             return unused
 
         lax.fori_loop(0, own_blocks // step_blocks, queries, 0)
-
-        def attend(b, best):
-            for k in range(len(across_from)):
-                pl.when((b == 2 * k) & (g + 1 < groups))(lambda k=k: forward(g + 1, k))
+        onward(2)
+
+        def attend(step, best):
+            b = lax.rem(other_chip * part + step, own_blocks)
             p = order[half * own_blocks + b]
             here = window(b, block)
             asking = label_ref[p]
@@ -526,13 +555,14 @@
                     jnp.bfloat16
                 )
                 out.append(jnp.maximum(best[head], top))
+            for k in range(3):
+                pl.when(step == (k + 1) * part)(lambda k=k: leave(g, k))
             return tuple(out)
 
         low = jnp.full((1, block), masked_value, jnp.float32)
         best = lax.fori_loop(0, own_blocks, attend, (low, low))
         peak_s[g] = jnp.concatenate(best, axis=0) * scale
-        start_all(context_copies(g))
-        kept_context(g).start()
+        leave(g, 3)
         return unused
 
     lax.fori_loop(0, groups, group, 0)
@@ -558,15 +588,15 @@
             for i in range(3):
                 target, arrived = w_spot(g, i, across_from[k] + d)
                 link(target, target, arrived, across, sent_x.at[g, i, k]).wait_send()
-        for copy in context_copies(g):
-            copy.wait_send()
-        kept_context(g).wait()
+        left(g)
         for k in range(1, quarter):
             arrive(*out_spot(g, first_of_half + lax.rem(place + k, quarter)))
         return unused
 
     lax.fori_loop(0, groups, settle, 0)
-    for copy, condition in started:
+    for k, (spot, where, condition) in enumerate(started):
+        target, arrived = spot()
+        copy = link(target, target, arrived, where, sent_l.at[k])
         if condition is None:
             copy.wait_send()
         else:
@@ -597,8 +627,6 @@
     angle = np.arange(count, dtype=np.float32)[:, None] * freqs[None, :]
     cosine, sine = np.cos(angle), np.sin(angle)
     turns = jnp.asarray(np.concatenate([cosine, cosine, -sine, sine], axis=1), jnp.float32)
-    every = jnp.arange(blocks, dtype=jnp.int32)
-    stored_at = jnp.sum(jnp.where(order[None, :] == every[:, None], every[None, :], 0), axis=1)
     bf, f32 = jnp.bfloat16, jnp.float32
     dma = pltpu.SemaphoreType.DMA
     context, peaks = pl.pallas_call(
@@ -607,7 +635,7 @@
             jax.ShapeDtypeStruct((rows, heads * VD), bf),
             jax.ShapeDtypeStruct((2 * devices, groups, 2, block), f32),
         ],
-        in_specs=[smem, smem, vmem] + [anyplace] * 7,
+        in_specs=[smem, vmem] + [anyplace] * 7,
         out_specs=[anyplace, vmem],
         scratch_shapes=[
             pltpu.VMEM((count // 2, sides * query_latent.shape[2]), bf),
@@ -627,6 +655,7 @@
             pltpu.VMEM((back + blocks, block, block), jnp.int32),
             pltpu.VMEM((blocks, block, 2 * ROPE), f32),
             pltpu.VMEM((groups, 2, block), f32),
+            pltpu.SMEM((blocks,), jnp.int32),
             dma((quarter, sides)),
             dma((devices, sides)),
             dma((devices,)),
@@ -637,7 +666,7 @@
             dma((groups, 3, quarter + 2)),
             dma((groups, 3, quarter - 1)),
             dma((groups, 3)),
-            dma((groups, quarter - 1)),
+            dma((groups, quarter)),
             dma((2 * devices,)),
             dma((5,)),
             dma((groups, 3)),
@@ -648,7 +677,7 @@
         ),
         name="fused",
     )(
-        order, stored_at, labels.reshape(blocks, 1, block), query_latent[0],
+        order, labels.reshape(blocks, 1, block), query_latent[0],
         key_latent[0].reshape(rows // block, block, key_latent.shape[2]),
         jnp.transpose(rope_key[0]), w_uq, w_uk, w_uv, turns.reshape(blocks, block, 2 * ROPE),
     )

time: 164 us -> 129 us (0.79)
  Pallas kernels: 156 us -> 121 us
    pallas_call x1, Pallas kernels: 156 us -> 121 us  [by_halves(): pl.pallas_call(functools.partial(fused, devices, block, groups), out_shap...]
where the time goes in v2:
time: 129 us; the launch traced here: 128 us
  Pallas kernels  121 us (94%)
  other arithmetic  3.78 us (3%)
  local copies, waits for them, and re-layouts  1.73 us (1%)
    pallas_call x1, Pallas kernels, by_halves(): pl.pallas_call(functools.partial(fused, devices, block, groups), out_shap...  121 us

profile of v2, /device:TPU:13, one launch (start us, length us, event | category | flops | bytes accessed | tf_op | source)
XLA Modules:
  0.0 127.7 jit_solution(14087668418327717032)
XLA Ops:
  0.6 0.0 copy-start
  0.6 121.5 %fused.1 = (bf16[256,4096]{1,0:T(8,128)(2,1)}, f32[16,4,2,128]{3,2,1,0:T(2,128)}) custom-call(s32[16]{0:T(128)} %bitcast.15, s32[16,1,128]{2,1,0:T(1,128)} %bitcast.14, bf16[256,768]{1,0:T(8,128)(2,1)} %bitcast.11, bf16[2,128,256]{2,1,0:T(8,128)(2,1)} %bitcast.12, bf16[64,256]{1,0:T(8,128)(2,1)} %bitcast.13, bf16[192,6144]{1,0:T(8,128)(2,1)} %uq_ref.1, ...), custom_call_target="tpu_custom_call" | custom-call | tf_op jit(solution)/shard_map/fused/pallas_call | solution.py:632
  122.1 1.0 reduce_max.10
  123.1 0.1 reduce_max.14
  123.3 0.1 broadcast_in_dim.8
  123.3 0.1 broadcast_in_dim.7
  123.4 0.1 mul.20
  123.5 0.0 copy-done
  123.5 0.0 copy-start.2
  123.5 0.0 copy-start.1
  123.5 1.9 %multiply_convert_fusion = bf16[192,6144]{1,0:T(8,128)(2,1)} fusion(bf16[192,6144]{1,0:T(8,128)(2,1)S(1)} %copy-done, f32[6144]{0:T(1024)S(1)} %mul.20), kind=kLoop, calls=%fused_computation | loop fusion | flops 3538944 | bytes 4743168 | tf_op jit(solution)/shard_map/convert_element_type | solution.py:698
  125.4 0.1 broadcast_bitcast_fusion
  125.5 0.0 copy-done.2
  125.5 0.9 multiply_convert_fusion.1
  126.4 0.0 copy-done.1
  126.4 1.3 %copy.13 = bf16[1,256,4096]{2,1,0:T(8,128)(2,1)} copy(bf16[1,256,4096]{2,1,0:T(8,128)(2,1)S(1)} %bitcast.10) | data formatting | bytes 4194304
  (3 shorter events, 0.0 us)
Async XLA Ops:
  0.6 122.9 %copy-start = (bf16[192,6144]{1,0:T(8,128)(2,1)S(1)}, bf16[192,6144]{1,0:T(8,128)(2,1)}, u32[]{:S(2)}) copy-start(bf16[192,6144]{1,0:T(8,128)(2,1)} %uq_ref.1) | copy-start | bytes 7077892
  123.5 2.0 %copy-start.2 = (bf16[64,4096]{1,0:T(8,128)(2,1)S(1)}, bf16[64,4096]{1,0:T(8,128)(2,1)}, u32[]{:S(2)}) copy-start(bf16[64,4096]{1,0:T(8,128)(2,1)} %uk_ref.1) | copy-start | bytes 1572868
  123.5 2.8 %copy-start.1 = (bf16[256,4096]{1,0:T(8,128)(2,1)S(1)}, bf16[256,4096]{1,0:T(8,128)(2,1)}, u32[]{:S(2)}) copy-start(bf16[256,4096]{1,0:T(8,128)(2,1)} %get-tuple-element.5) | copy-start | bytes 6291460

commit v3 on v2

--- a/solution.py
+++ b/solution.py
@@ -171,7 +171,7 @@
     n, block, groups,
     order, label_ref, query_ref, key_ref, rope_ref, uq_ref, uk_ref, uv_ref, turn_ref,
     out_ref, peaks_ref,
-    q_lat, k_lat, r_lat, r_blk, wq_s, wk_s, wv_s, wvt_s, q_s, k_s, vt_s, s_s, p_s, c_s, lab_s, turn_s,
+    q_lat, k_lat, r_lat, r_blk, wq_s, wk_s, wv_s, wvt_s, wide_s, q_s, k_s, vt_s, s_s, p_s, c_s, lab_s, turn_s,
     peak_s, inv_s,
     got_q, got_k, got_r, got_w, got_c, got_p,
     sent_l, sent_w, sent_x, sent_m, sent_c, sent_p, local_l, local_w, local_c,
@@ -266,8 +266,8 @@
     near_to = [pair_chip, pair_chip + 1]
     sender = core == d
 
-    def far_copies(g):
-        return [w_copy(g, i, k, to) for k, to in enumerate(far_to) for i in range(3)]
+    def far_copies(g, first=0):
+        return [w_copy(g, i, k, far_to[k]) for k in range(first, first + 2) for i in range(3)]
 
     def near_copies(g):
         return [w_copy(g, i, quarter + k, to) for k, to in enumerate(near_to) for i in range(3)]
@@ -277,10 +277,13 @@
             copy.start()
 
     def send_weights(g):
-        start_all(near_copies(g) + far_copies(g))
+        start_all(near_copies(g) + far_copies(g, 0))
+        pl.when(~inner)(lambda: start_all(far_copies(g, 2)))
+        pl.when(inner & (g + 1 < groups))(lambda: start_all(far_copies(g + 1, 2)))
 
     pl.when(sender & ~inner)(lambda: start_all(near_copies(0)))
-    pl.when(sender)(lambda: start_all(far_copies(0)))
+    pl.when(sender)(lambda: start_all(far_copies(0, 0) + far_copies(0, 2)))
+    pl.when(sender & inner)(lambda: start_all(far_copies(1, 2)))
 
 
     def mate_copies(g):
@@ -413,6 +416,7 @@
         arrive(*q_spot(src, 1 - t))
 
     step_blocks = 4
+    devices_rows = uq_ref.shape[0]
     chunk = step_blocks * block
     factor = scale * math.log2(math.e)
 
@@ -449,19 +453,36 @@
             pl.when(core != k - 2)(context_to(g, k).wait_send)
         kept_context(g).wait()
 
+    held = inner & ~sender
+    onward_at = ("keys", "queries", 1)
+
     def group(g, unused):
         pl.when(sender & (g + 3 < groups))(lambda: send_weights(g + 3))
-        for k in range(len(across_from)):
-            for i in range(3):
+        def await_weights(i):
+            for k in range(len(across_from)):
                 arrive(*w_spot(g, i, across_from[k] + 1 - d))
-        for i in range(3):
             arrive(*w_spot(g, i, mate))
-        for copy in kept_weights(g):
-            copy.wait()
-
-        def onward(k):
-            pl.when(g + 1 < groups)(lambda: forward(g + 1, k))
-
+            kept_weights(g)[i].wait()
+
+        for i in range(2):
+            await_weights(i)
+
+        def onward(where):
+            for k in range(3):
+                if onward_at[k] == where:
+                    pl.when(g + 1 < groups)(lambda k=k: forward(g + 1, k))
+
+        @pl.when(held & (g >= 2))
+        def _():
+            for k in range(2):
+                leave(g - 2, k)
+
+        @pl.when(held & (g + 1 == groups))
+        def _():
+            for k in range(2):
+                leave(g - 1, k)
+
+        onward("start")
         wvt_s[...] = jnp.transpose(wv_s[g])
 
         def keys(step, unused):
@@ -481,39 +502,59 @@
                 vt_s[at] = value[:, lo:hi]
             return unused
 
-        onward(0)
         lax.fori_loop(0, blocks // step_blocks, keys, 0)
-        onward(1)
+        onward("keys")
+
+        def widen(step, unused):
+            here = window(step, devices_rows)
+            raw = wq_s[g, here, :]
+            pieces = []
+            for head in range(2):
+                base = head * turn_width
+                rope = base + NOPE
+                middle = rope + ROPE // 2
+                pieces += [
+                    raw[:, base:rope], raw[:, rope : rope + ROPE],
+                    raw[:, middle : rope + ROPE], raw[:, rope:middle],
+                ]
+            wide_s[here, :] = jnp.concatenate(pieces, axis=1)
+            return unused
+
+        await_weights(2)
+        lax.fori_loop(0, n, widen, 0)
 
         def queries(step, unused):
             full = jnp.dot(
-                q_lat[window(step, chunk), :], wq_s[g], preferred_element_type=jnp.float32
+                q_lat[window(step, chunk), :], wide_s[...], preferred_element_type=jnp.float32
             )
             for j in range(step_blocks):
                 b = step * step_blocks + j
                 turns = turn_s[order[half * own_blocks + b]]
-                cosine, sine = turns[:, :ROPE], turns[:, ROPE:]
                 lo, hi = j * block, (j + 1) * block
                 here = window(b, block)
                 for head in range(2):
-                    base = head * turn_width
+                    base = head * 2 * NOPE
                     q_s[head, here, :NOPE] = full[lo:hi, base : base + NOPE].astype(jnp.bfloat16)
-                    q_s[head, here, NOPE:] = turned(
-                        full[lo:hi, base + NOPE : base + turn_width], cosine, sine
-                    ).astype(jnp.bfloat16)
+                    both = full[lo:hi, base + NOPE : base + 2 * NOPE] * turns
+                    q_s[head, here, NOPE:] = (both[:, :ROPE] + both[:, ROPE:]).astype(
+                        jnp.bfloat16
+                    )
             return unused
 
         lax.fori_loop(0, own_blocks // step_blocks, queries, 0)
-        onward(2)
-
-        def attend(step, best):
+        onward("queries")
+
+        causal = lax.broadcasted_iota(jnp.int32, (block, block), 0) <= (
+            lax.broadcasted_iota(jnp.int32, (block, block), 1)
+        )
+
+        def place_of(step):
             b = lax.rem(other_chip * part + step, own_blocks)
-            p = order[half * own_blocks + b]
-            here = window(b, block)
+            return window(b, block), order[half * own_blocks + b]
+
+        def score(step, slot):
+            here, p = place_of(step)
             asking = label_ref[p]
-            causal = lax.broadcasted_iota(jnp.int32, (block, block), 0) <= (
-                lax.broadcasted_iota(jnp.int32, (block, block), 1)
-            )
             raws = [
                 lax.dot_general(
                     jnp.concatenate([k_s[head, p + j] for j in range(back + 1)], axis=0),
@@ -530,39 +571,61 @@
                     allowed = allowed & causal
                 for head in range(2):
                     raw = jnp.where(allowed, raws[head][lo:hi, :], masked_value)
-                    s_s[head, lo:hi, :] = raw
+                    s_s[slot, head, lo:hi, :] = raw
                     tops[head] = jnp.maximum(
                         tops[head], jnp.max(raw.reshape(block // 8, 8, block), axis=0)
                     )
-            out = []
+            return tuple(jnp.max(tops[head], axis=0, keepdims=True) for head in range(2))
+
+        def mix(step, slot, tops, best):
+            here, p = place_of(step)
             for head in range(2):
-                top = jnp.max(tops[head], axis=0, keepdims=True)
+                top = tops[head]
                 total = jnp.zeros((8, block), jnp.float32)
                 for j in range(back + 1):
                     lo, hi = j * block, (j + 1) * block
-                    piece = jnp.exp2((s_s[head, lo:hi, :] - top) * factor)
+                    piece = jnp.exp2((s_s[slot, head, lo:hi, :] - top) * factor)
                     total = total + jnp.sum(piece.reshape(block // 8, 8, block), axis=0)
-                    p_s[head, lo:hi, :] = piece.astype(jnp.bfloat16)
+                    p_s[slot, head, lo:hi, :] = piece.astype(jnp.bfloat16)
                 mixed = jnp.dot(
                     jnp.concatenate(
                         [vt_s[p + j, head * VD : (head + 1) * VD, :] for j in range(back + 1)], axis=1
                     ),
-                    p_s[head],
+                    p_s[slot, head],
                     preferred_element_type=jnp.float32,
                 )
                 done = mixed / jnp.sum(total, axis=0, keepdims=True)
                 c_s[g, here, head * VD : (head + 1) * VD] = jnp.transpose(done).astype(
                     jnp.bfloat16
                 )
-                out.append(jnp.maximum(best[head], top))
+            return tuple(jnp.maximum(best[head], tops[head]) for head in range(2))
+
+        def attend(turn, carried):
+            tops, best = carried
+            for slot in range(2):
+                step = 2 * turn + slot
+                later = score(step + 1, 1 - slot)
+                best = mix(step, slot, tops, best)
+                tops = later
+            for k in range(2):
+                pl.when((turn == k + 1) & (~held | (g + 1 == groups)))(lambda k=k: leave(g, k))
             for k in range(3):
-                pl.when(step == (k + 1) * part)(lambda k=k: leave(g, k))
-            return tuple(out)
+                at = onward_at[k]
+                if isinstance(at, int):
+                    pl.when((turn == at) & (g + 1 < groups))(lambda k=k: forward(g + 1, k))
+            return (tops, best)
 
         low = jnp.full((1, block), masked_value, jnp.float32)
-        best = lax.fori_loop(0, own_blocks, attend, (low, low))
+        rounds = own_blocks // 2 - 1
+        tops, best = lax.fori_loop(0, rounds, attend, (score(0, 0), (low, low)))
+        onward("six")
+        later = score(2 * rounds + 1, 1)
+        best = mix(2 * rounds, 0, tops, best)
+        leave(g, 2)
+        best = mix(2 * rounds + 1, 1, later, best)
         peak_s[g] = jnp.concatenate(best, axis=0) * scale
         leave(g, 3)
+        onward("end")
         return unused
 
     lax.fori_loop(0, groups, group, 0)
@@ -578,7 +641,7 @@
 
     def settle(g, unused):
         def far_sent():
-            for copy in far_copies(g) + near_copies(g):
+            for copy in far_copies(g, 0) + far_copies(g, 2) + near_copies(g):
                 copy.wait_send()
 
         pl.when(sender)(far_sent)
@@ -628,15 +691,17 @@
     cosine, sine = np.cos(angle), np.sin(angle)
     turns = jnp.asarray(np.concatenate([cosine, cosine, -sine, sine], axis=1), jnp.float32)
     bf, f32 = jnp.bfloat16, jnp.float32
+    beside = 2 * (rows * heads * VD + w_uq.size + w_uk.size) + 8 * devices * groups * 2 * block
+    grant = 67043328 - beside - 384 * 1024
     dma = pltpu.SemaphoreType.DMA
     context, peaks = pl.pallas_call(
         functools.partial(fused, devices, block, groups),
         out_shape=[
-            jax.ShapeDtypeStruct((rows, heads * VD), bf),
-            jax.ShapeDtypeStruct((2 * devices, groups, 2, block), f32),
+            pltpu.VMEM((rows, heads * VD), bf),
+            pltpu.VMEM((2 * devices, groups, 2, block), f32),
         ],
         in_specs=[smem, vmem] + [anyplace] * 7,
-        out_specs=[anyplace, vmem],
+        out_specs=[vmem, vmem],
         scratch_shapes=[
             pltpu.VMEM((count // 2, sides * query_latent.shape[2]), bf),
             pltpu.VMEM((blocks, block, sides * key_latent.shape[2]), bf),
@@ -646,11 +711,12 @@
             pltpu.VMEM((groups, devices * w_uk.shape[0], 2 * NOPE), bf),
             pltpu.VMEM((groups, devices * w_uv.shape[0], 2 * VD), bf),
             pltpu.VMEM((2 * VD, devices * w_uv.shape[0]), bf),
+            pltpu.VMEM((devices * w_uq.shape[0], 4 * NOPE), bf),
             pltpu.VMEM((2, count // 2, NOPE + ROPE), bf),
             pltpu.VMEM((2, back + blocks, block, NOPE + ROPE), bf),
             pltpu.VMEM((back + blocks, 2 * VD, block), bf),
-            pltpu.VMEM((2, (back + 1) * block, block), f32),
-            pltpu.VMEM((2, (back + 1) * block, block), bf),
+            pltpu.VMEM((2, 2, (back + 1) * block, block), f32),
+            pltpu.VMEM((2, 2, (back + 1) * block, block), bf),
             pltpu.VMEM((groups, count // 2, 2 * VD), bf),
             pltpu.VMEM((back + blocks, block, block), jnp.int32),
             pltpu.VMEM((blocks, block, 2 * ROPE), f32),
@@ -673,7 +739,7 @@
             dma((groups,)),
         ],
         compiler_params=pltpu.CompilerParams(
-            collective_id=0, has_side_effects=True, vmem_limit_bytes=60 * 1024 * 1024
+            collective_id=0, has_side_effects=True, vmem_limit_bytes=grant
         ),
         name="fused",
     )(
@@ -681,8 +747,73 @@
         key_latent[0].reshape(rows // block, block, key_latent.shape[2]),
         jnp.transpose(rope_key[0]), w_uq, w_uk, w_uv, turns.reshape(blocks, block, 2 * ROPE),
     )
-    head_max = jnp.max(peaks.reshape(2, 2, heads, block), axis=(0, 1, 3))
-    return (context[None],) + clipped(w_uq, w_uk, head_max, heads)
+    parts = 4
+    context, clipped_uq, clipped_uk = pl.pallas_call(
+        functools.partial(finish, parts, quarter),
+        out_shape=[
+            jax.ShapeDtypeStruct((rows, heads * VD), bf),
+            jax.ShapeDtypeStruct(w_uq.shape, bf),
+            jax.ShapeDtypeStruct(w_uk.shape, bf),
+        ],
+        in_specs=[vmem] * 4,
+        out_specs=[anyplace] * 3,
+        scratch_shapes=[
+            pltpu.VMEM(w_uq.shape, bf),
+            pltpu.VMEM(w_uk.shape, bf),
+            dma((parts,)),
+            dma((quarter, 2)),
+        ],
+        compiler_params=pltpu.CompilerParams(vmem_limit_bytes=24 * 1024 * 1024),
+        name="finish",
+    )(context, peaks.reshape(2 * devices, 2 * groups, block), w_uq, w_uk)
+    return (context[None], clipped_uq, clipped_uk)
+
+
+def finish(
+    parts, quarter, context_ref, peak_ref, uq_ref, uk_ref, out_ref, cq_ref, ck_ref,
+    cq_s, ck_s, gone, done,
+):
+    size = context_ref.shape[0] // parts
+    places = [pl.ds(k * size, size) for k in range(parts)]
+    go = [
+        pltpu.make_async_copy(context_ref.at[at, :], out_ref.at[at, :], gone.at[k])
+        for k, at in enumerate(places)
+    ]
+    for copy in go:
+        copy.start()
+    own = peak_ref.shape[1]
+    lane = lax.broadcasted_iota(jnp.int32, (1, 128), 1)
+    wide, thin = own * (NOPE + ROPE), own * NOPE
+    sent = []
+    for j in range(quarter):
+        top = peak_ref[j]
+        for k in range(1, peak_ref.shape[0] // quarter):
+            top = jnp.maximum(top, peak_ref[j + k * quarter])
+        ratio = CLIP / jnp.maximum(jnp.max(top, axis=1, keepdims=True), CLIP)
+        root = jnp.broadcast_to(jnp.sqrt(ratio), (own, 128))
+        ratio = jnp.broadcast_to(ratio, (own, 128))
+        for head in range(0, own, 2):
+            root_0, root_1 = root[head : head + 1], root[head + 1 : head + 2]
+            ratio_0, ratio_1 = ratio[head : head + 1], ratio[head + 1 : head + 2]
+            factors = [
+                root_0,
+                jnp.where(lane < ROPE, ratio_0, root_1),
+                jnp.where(lane < ROPE, root_1, ratio_1),
+            ]
+            base = j * wide + head * (NOPE + ROPE)
+            for k in range(3):
+                at = slice(base + k * 128, base + (k + 1) * 128)
+                cq_s[:, at] = (uq_ref[:, at].astype(jnp.float32) * factors[k]).astype(jnp.bfloat16)
+            for k, factor in enumerate((root_0, root_1)):
+                at = slice(j * thin + (head + k) * NOPE, j * thin + (head + k + 1) * NOPE)
+                ck_s[:, at] = (uk_ref[:, at].astype(jnp.float32) * factor).astype(jnp.bfloat16)
+        for k, (source, target, width) in enumerate(((cq_s, cq_ref, wide), (ck_s, ck_ref, thin))):
+            at = pl.ds(j * width, width)
+            copy = pltpu.make_async_copy(source.at[:, at], target.at[:, at], done.at[j, k])
+            copy.start()
+            sent.append(copy)
+    for copy in sent + go:
+        copy.wait()
 
 
 def clipped(w_uq, w_uk, head_max, heads):
@@ -703,7 +834,7 @@
 def on_device(*arrays):
     heads = arrays[3].shape[1] // (NOPE + ROPE)
     pairs = lax.axis_size("tp") == 2 and lax.axis_size("dp") == 2
-    if pairs and lax.axis_size("seq") == 8 and heads % 8 == 0:
+    if pairs and lax.axis_size("seq") == 8 and heads % 8 == 0 and heads >= 16:
         return by_halves(*arrays)
     return by_tokens(*arrays)
 

time: 129 us -> 120 us (0.930)
  Pallas kernels: 121 us -> 117 us
  other arithmetic: 3.78 us -> 0 us
  local copies, waits for them, and re-layouts: 1.73 us -> 0.01 us
    pallas_call x1, Pallas kernels: 121 us -> 115 us  [by_halves(): pl.pallas_call(functools.partial(fused, devices, block, groups), out_shap...]
    convert_element_type x2 -> x0, other arithmetic: 2.75 us -> none  [the longest x1 1.86 us: clipped(): (w_uq.astype(jnp.float32) * factors[None, :]).astype(jnp.bfloat16)]
    pallas_call x0 -> x1, Pallas kernels: none -> 2.44 us  [by_halves(): pl.pallas_call(functools.partial(finish, parts, quarter), out_shape=[jax....]
    unnamed x7 -> x4, local copies, waits for them, and re-layouts: 1.33 us -> 0.01 us
where the time goes in v3:
time: 120 us; the launch traced here: 118 us
  Pallas kernels  117 us (98%)
    pallas_call x1, Pallas kernels, by_halves(): pl.pallas_call(functools.partial(fused, devices, block, groups), out_shap...  115 us
    pallas_call x1, Pallas kernels, by_halves(): pl.pallas_call(functools.partial(finish, parts, quarter), out_shape=[jax....  2.44 us

profile of v3, /device:TPU:13, one launch (start us, length us, event | category | flops | bytes accessed | tf_op | source)
XLA Modules:
  0.0 117.9 jit_solution(1100838932350045145)
XLA Ops:
  0.6 0.0 copy-start
  0.6 0.0 copy-start.1
  0.7 114.8 %fused.1 = (bf16[256,4096]{1,0:T(8,128)(2,1)S(1)}, f32[16,4,2,128]{3,2,1,0:T(2,128)S(1)}) custom-call(s32[16]{0:T(128)} %bitcast.14, s32[16,1,128]{2,1,0:T(1,128)} %bitcast.13, bf16[256,768]{1,0:T(8,128)(2,1)} %bitcast.10, bf16[2,128,256]{2,1,0:T(8,128)(2,1)} %bitcast.11, bf16[64,256]{1,0:T(8,128)(2,1)} %bitcast.12, bf16[192,6144]{1,0:T(8,128)(2,1)} %uq_ref.3, ...), custom_call_target="tpu_custom_call" | custom-call | tf_op jit(solution)/shard_map/fused/pallas_call | solution.py:697
  115.5 0.0 copy-done
  115.5 0.0 copy-done.1
  115.5 2.4 %finish.1 = (bf16[256,4096]{1,0:T(8,128)(2,1)}, bf16[192,6144]{1,0:T(8,128)(2,1)}, bf16[64,4096]{1,0:T(8,128)(2,1)}) custom-call(bf16[256,4096]{1,0:T(8,128)(2,1)S(1)} %get-tuple-element.8.context_ref, f32[16,8,128]{2,1,0:T(8,128)S(1)} %bitcast.9, bf16[192,6144]{1,0:T(8,128)(2,1)S(1)} %copy-done, bf16[64,4096]{1,0:T(8,128)(2,1)S(1)} %copy-done.1), custom_call_target="tpu_custom_call" | custom-call | tf_op jit(solution)/shard_map/finish/pallas_call | solution.py:751
Async XLA Ops:
  0.6 114.8 %copy-start = (bf16[192,6144]{1,0:T(8,128)(2,1)S(1)}, bf16[192,6144]{1,0:T(8,128)(2,1)}, u32[]{:S(2)}) copy-start(bf16[192,6144]{1,0:T(8,128)(2,1)} %uq_ref.3) | copy-start | bytes 7077892
  0.6 114.8 %copy-start.1 = (bf16[64,4096]{1,0:T(8,128)(2,1)S(1)}, bf16[64,4096]{1,0:T(8,128)(2,1)}, u32[]{:S(2)}) copy-start(bf16[64,4096]{1,0:T(8,128)(2,1)} %uk_ref.3) | copy-start | bytes 1572868

commit v4 on v3

--- a/solution.py
+++ b/solution.py
@@ -171,7 +171,7 @@
     n, block, groups,
     order, label_ref, query_ref, key_ref, rope_ref, uq_ref, uk_ref, uv_ref, turn_ref,
     out_ref, peaks_ref,
-    q_lat, k_lat, r_lat, r_blk, wq_s, wk_s, wv_s, wvt_s, wide_s, q_s, k_s, vt_s, s_s, p_s, c_s, lab_s, turn_s,
+    q_lat, k_lat, r_lat, r_blk, wq_s, wk_s, wv_s, wvt_s, q_s, k_s, vt_s, s_s, p_s, c_s, lab_s, turn_s,
     peak_s, inv_s,
     got_q, got_k, got_r, got_w, got_c, got_p,
     sent_l, sent_w, sent_x, sent_m, sent_c, sent_p, local_l, local_w, local_c,
@@ -200,7 +200,9 @@
     own_blocks = blocks // 2
     back = blocks // 2
     scale = 1.0 / math.sqrt(NOPE + ROPE)
-    turn_width = NOPE + ROPE
+    lane = lax.broadcasted_iota(jnp.int32, (block, 2 * ROPE), 1)
+    quarter_turn = lax.rem(lane, ROPE) < ROPE // 2
+    low_lane = lane < ROPE
 
     def link(source, target, arrived, where, sender):
         return pltpu.make_async_remote_copy(
@@ -327,7 +329,7 @@
     def empty_step(p, unused):
         lab_s[p] = jnp.full((block, block), -1, jnp.int32)
         for head in range(2):
-            k_s[head, p] = jnp.zeros((block, turn_width), jnp.bfloat16)
+            k_s[head, p] = jnp.zeros((block, NOPE + 2 * ROPE), jnp.bfloat16)
         vt_s[p] = jnp.zeros((2 * VD, block), jnp.bfloat16)
         return unused
 
@@ -351,15 +353,22 @@
         arrive(*q_spot(src, 1 - t))
         send(None, lambda: q_spot(src, 1 - t), to_mate)
 
+    def turned_pair(values, turns):
+        swapped = jnp.where(
+            quarter_turn,
+            pltpu.roll(values, 2 * ROPE - ROPE // 2, 1), pltpu.roll(values, ROPE // 2, 1),
+        )
+        return values * turns[:, : 2 * ROPE] + swapped * turns[:, 2 * ROPE :]
+
     def turn_ropes():
         for b in range(blocks):
             r_blk[b] = r_lat[:, b * block : (b + 1) * block]
 
         def rope_step(p, unused):
-            raw = jnp.transpose(r_blk[inv_s[p]].astype(jnp.float32))
-            turned_key = turned(raw, turn_s[p, :, :ROPE], turn_s[p, :, ROPE:]).astype(jnp.bfloat16)
+            raw = r_blk[inv_s[p]].astype(jnp.float32)
+            both = turned_pair(jnp.transpose(jnp.concatenate([raw, raw], axis=0)), turn_s[p])
             for head in range(2):
-                k_s[head, p + back, :, NOPE:] = turned_key
+                k_s[head, p + back, :, NOPE:] = both.astype(jnp.bfloat16)
             return unused
 
         lax.fori_loop(0, blocks, rope_step, 0)
@@ -395,14 +404,11 @@
     hand_keys(pair)
     forward(0, 1)
     pl.when(sender)(lambda: send_weights(1))
-    forward(0, 2)
     under(~inner, take)
     for src in far:
         hand_keys(src)
+    forward(0, 2)
     hand_query(pair)
-    forward(0, 0)
-    pl.when(sender)(lambda: send_weights(2))
-
     for k in range(quarter):
         src = 2 * k + 1 - core
         arrive(*k_spot(src, t))
@@ -411,12 +417,13 @@
     for copy in kept:
         copy.wait()
     turn_ropes()
+    forward(0, 0)
+    pl.when(sender)(lambda: send_weights(2))
     for src in (mate, pair + 1 - 2 * core):
         arrive(*q_spot(src, t))
         arrive(*q_spot(src, 1 - t))
 
     step_blocks = 4
-    devices_rows = uq_ref.shape[0]
     chunk = step_blocks * block
     factor = scale * math.log2(math.e)
 
@@ -490,7 +497,7 @@
                 [k_lat[inv_s[step * step_blocks + j]] for j in range(step_blocks)], axis=0
             )
             nope = jnp.dot(latent, wk_s[g], preferred_element_type=jnp.float32)
-            nope = nope.astype(jnp.bfloat16)
+            nope = (nope[:, :NOPE], pltpu.roll(nope[:, NOPE:], ROPE, 1))
             value = lax.dot_general(
                 wvt_s[...], latent, (((1,), (1,)), ((), ())), preferred_element_type=jnp.float32
             )
@@ -498,49 +505,31 @@
             for j in range(step_blocks):
                 at, lo, hi = back + step * step_blocks + j, j * block, (j + 1) * block
                 for head in range(2):
-                    k_s[head, at, :, :NOPE] = nope[lo:hi, head * NOPE : (head + 1) * NOPE]
+                    k_s[head, at, :, :NOPE] = nope[head][lo:hi, :].astype(jnp.bfloat16)
                 vt_s[at] = value[:, lo:hi]
             return unused
 
         lax.fori_loop(0, blocks // step_blocks, keys, 0)
         onward("keys")
 
-        def widen(step, unused):
-            here = window(step, devices_rows)
-            raw = wq_s[g, here, :]
-            pieces = []
-            for head in range(2):
-                base = head * turn_width
-                rope = base + NOPE
-                middle = rope + ROPE // 2
-                pieces += [
-                    raw[:, base:rope], raw[:, rope : rope + ROPE],
-                    raw[:, middle : rope + ROPE], raw[:, rope:middle],
-                ]
-            wide_s[here, :] = jnp.concatenate(pieces, axis=1)
-            return unused
-
-        await_weights(2)
-        lax.fori_loop(0, n, widen, 0)
-
         def queries(step, unused):
             full = jnp.dot(
-                q_lat[window(step, chunk), :], wide_s[...], preferred_element_type=jnp.float32
+                q_lat[window(step, chunk), :], wq_s[g], preferred_element_type=jnp.float32
             )
             for j in range(step_blocks):
                 b = step * step_blocks + j
                 turns = turn_s[order[half * own_blocks + b]]
                 lo, hi = j * block, (j + 1) * block
                 here = window(b, block)
-                for head in range(2):
-                    base = head * 2 * NOPE
-                    q_s[head, here, :NOPE] = full[lo:hi, base : base + NOPE].astype(jnp.bfloat16)
-                    both = full[lo:hi, base + NOPE : base + 2 * NOPE] * turns
-                    q_s[head, here, NOPE:] = (both[:, :ROPE] + both[:, ROPE:]).astype(
-                        jnp.bfloat16
-                    )
+                first, second, third = (full[lo:hi, k * NOPE : (k + 1) * NOPE] for k in range(3))
+                ropes = turned_pair(jnp.where(low_lane, second, third), turns)
+                q_s[0, here, :NOPE] = first.astype(jnp.bfloat16)
+                q_s[1, here, :NOPE] = jnp.where(low_lane, third, second).astype(jnp.bfloat16)
+                q_s[0, here, NOPE:] = jnp.where(low_lane, ropes, 0.0).astype(jnp.bfloat16)
+                q_s[1, here, NOPE:] = jnp.where(low_lane, 0.0, ropes).astype(jnp.bfloat16)
             return unused
 
+        await_weights(2)
         lax.fori_loop(0, own_blocks // step_blocks, queries, 0)
         onward("queries")
 
@@ -689,7 +678,8 @@
     freqs = np.exp(np.float32(-math.log(rope_base)) * steps).astype(np.float32)
     angle = np.arange(count, dtype=np.float32)[:, None] * freqs[None, :]
     cosine, sine = np.cos(angle), np.sin(angle)
-    turns = jnp.asarray(np.concatenate([cosine, cosine, -sine, sine], axis=1), jnp.float32)
+    table = [cosine] * 4 + [-sine, sine] * 2
+    turns = jnp.asarray(np.concatenate(table, axis=1), jnp.float32)
     bf, f32 = jnp.bfloat16, jnp.float32
     beside = 2 * (rows * heads * VD + w_uq.size + w_uk.size) + 8 * devices * groups * 2 * block
     grant = 67043328 - beside - 384 * 1024
@@ -711,15 +701,14 @@
             pltpu.VMEM((groups, devices * w_uk.shape[0], 2 * NOPE), bf),
             pltpu.VMEM((groups, devices * w_uv.shape[0], 2 * VD), bf),
             pltpu.VMEM((2 * VD, devices * w_uv.shape[0]), bf),
-            pltpu.VMEM((devices * w_uq.shape[0], 4 * NOPE), bf),
-            pltpu.VMEM((2, count // 2, NOPE + ROPE), bf),
-            pltpu.VMEM((2, back + blocks, block, NOPE + ROPE), bf),
+            pltpu.VMEM((2, count // 2, NOPE + 2 * ROPE), bf),
+            pltpu.VMEM((2, back + blocks, block, NOPE + 2 * ROPE), bf),
             pltpu.VMEM((back + blocks, 2 * VD, block), bf),
             pltpu.VMEM((2, 2, (back + 1) * block, block), f32),
             pltpu.VMEM((2, 2, (back + 1) * block, block), bf),
             pltpu.VMEM((groups, count // 2, 2 * VD), bf),
             pltpu.VMEM((back + blocks, block, block), jnp.int32),
-            pltpu.VMEM((blocks, block, 2 * ROPE), f32),
+            pltpu.VMEM((blocks, block, 4 * ROPE), f32),
             pltpu.VMEM((groups, 2, block), f32),
             pltpu.SMEM((blocks,), jnp.int32),
             dma((quarter, sides)),
@@ -745,7 +734,7 @@
     )(
         order, labels.reshape(blocks, 1, block), query_latent[0],
         key_latent[0].reshape(rows // block, block, key_latent.shape[2]),
-        jnp.transpose(rope_key[0]), w_uq, w_uk, w_uv, turns.reshape(blocks, block, 2 * ROPE),
+        jnp.transpose(rope_key[0]), w_uq, w_uk, w_uv, turns.reshape(blocks, block, 4 * ROPE),
     )
     parts = 4
     context, clipped_uq, clipped_uk = pl.pallas_call(

time: 120 us -> 119 us (level)
  no operation moved by 1% of the time
where the time goes in v4:
time: 119 us; the launch traced here: 117 us
  Pallas kernels  116 us (97%)
    pallas_call x1, Pallas kernels, by_halves(): pl.pallas_call(functools.partial(fused, devices, block, groups), out_shap...  114 us
    pallas_call x1, Pallas kernels, by_halves(): pl.pallas_call(functools.partial(finish, parts, quarter), out_shape=[jax....  2.44 us

profile of v4, /device:TPU:13, one launch (start us, length us, event | category | flops | bytes accessed | tf_op | source)
XLA Modules:
  0.0 116.7 jit_solution(10568057283219556478)
XLA Ops:
  0.6 0.0 copy-start
  0.6 0.0 copy-start.1
  0.7 113.6 %fused.1 = (bf16[256,4096]{1,0:T(8,128)(2,1)S(1)}, f32[16,4,2,128]{3,2,1,0:T(2,128)S(1)}) custom-call(s32[16]{0:T(128)} %bitcast.14, s32[16,1,128]{2,1,0:T(1,128)} %bitcast.13, bf16[256,768]{1,0:T(8,128)(2,1)} %bitcast.10, bf16[2,128,256]{2,1,0:T(8,128)(2,1)} %bitcast.11, bf16[64,256]{1,0:T(8,128)(2,1)} %bitcast.12, bf16[192,6144]{1,0:T(8,128)(2,1)} %uq_ref.3, ...), custom_call_target="tpu_custom_call" | custom-call | tf_op jit(solution)/shard_map/fused/pallas_call | solution.py:687
  114.3 0.0 copy-done
  114.3 0.0 copy-done.1
  114.3 2.4 %finish.1 = (bf16[256,4096]{1,0:T(8,128)(2,1)}, bf16[192,6144]{1,0:T(8,128)(2,1)}, bf16[64,4096]{1,0:T(8,128)(2,1)}) custom-call(bf16[256,4096]{1,0:T(8,128)(2,1)S(1)} %get-tuple-element.8.context_ref, f32[16,8,128]{2,1,0:T(8,128)S(1)} %bitcast.9, bf16[192,6144]{1,0:T(8,128)(2,1)S(1)} %copy-done, bf16[64,4096]{1,0:T(8,128)(2,1)S(1)} %copy-done.1), custom_call_target="tpu_custom_call" | custom-call | tf_op jit(solution)/shard_map/finish/pallas_call | solution.py:740
Async XLA Ops:
  0.6 113.7 %copy-start = (bf16[192,6144]{1,0:T(8,128)(2,1)S(1)}, bf16[192,6144]{1,0:T(8,128)(2,1)}, u32[]{:S(2)}) copy-start(bf16[192,6144]{1,0:T(8,128)(2,1)} %uq_ref.3) | copy-start | bytes 7077892
  0.6 113.7 %copy-start.1 = (bf16[64,4096]{1,0:T(8,128)(2,1)S(1)}, bf16[64,4096]{1,0:T(8,128)(2,1)}, u32[]{:S(2)}) copy-start(bf16[64,4096]{1,0:T(8,128)(2,1)} %uk_ref.3) | copy-start | bytes 1572868

commit v5 on v4

--- a/solution.py
+++ b/solution.py
@@ -418,7 +418,6 @@
         copy.wait()
     turn_ropes()
     forward(0, 0)
-    pl.when(sender)(lambda: send_weights(2))
     for src in (mate, pair + 1 - 2 * core):
         arrive(*q_spot(src, t))
         arrive(*q_spot(src, 1 - t))
@@ -464,7 +463,7 @@
     onward_at = ("keys", "queries", 1)
 
     def group(g, unused):
-        pl.when(sender & (g + 3 < groups))(lambda: send_weights(g + 3))
+        pl.when(sender & (g + 2 < groups))(lambda: send_weights(g + 2))
         def await_weights(i):
             for k in range(len(across_from)):
                 arrive(*w_spot(g, i, across_from[k] + 1 - d))

time: 119 us -> 117 us (0.983)
  Pallas kernels: 116 us -> 114 us
    pallas_call x1, Pallas kernels: 114 us -> 111 us  [by_halves(): pl.pallas_call(functools.partial(fused, devices, block, groups), out_shap...]
where the time goes in v5:
time: 117 us; the launch traced here: 114 us
  Pallas kernels  114 us (97%)
    pallas_call x1, Pallas kernels, by_halves(): pl.pallas_call(functools.partial(fused, devices, block, groups), out_shap...  111 us
    pallas_call x1, Pallas kernels, by_halves(): pl.pallas_call(functools.partial(finish, parts, quarter), out_shape=[jax....  2.44 us

profile of v5, /device:TPU:13, one launch (start us, length us, event | category | flops | bytes accessed | tf_op | source)
XLA Modules:
  0.0 114.2 jit_solution(17663154829666506502)
XLA Ops:
  0.6 0.0 copy-start
  0.6 0.0 copy-start.1
  0.7 111.1 %fused.1 = (bf16[256,4096]{1,0:T(8,128)(2,1)S(1)}, f32[16,4,2,128]{3,2,1,0:T(2,128)S(1)}) custom-call(s32[16]{0:T(128)} %bitcast.14, s32[16,1,128]{2,1,0:T(1,128)} %bitcast.13, bf16[256,768]{1,0:T(8,128)(2,1)} %bitcast.10, bf16[2,128,256]{2,1,0:T(8,128)(2,1)} %bitcast.11, bf16[64,256]{1,0:T(8,128)(2,1)} %bitcast.12, bf16[192,6144]{1,0:T(8,128)(2,1)} %uq_ref.3, ...), custom_call_target="tpu_custom_call" | custom-call | tf_op jit(solution)/shard_map/fused/pallas_call | solution.py:686
  111.7 0.0 copy-done
  111.8 0.0 copy-done.1
  111.8 2.4 %finish.1 = (bf16[256,4096]{1,0:T(8,128)(2,1)}, bf16[192,6144]{1,0:T(8,128)(2,1)}, bf16[64,4096]{1,0:T(8,128)(2,1)}) custom-call(bf16[256,4096]{1,0:T(8,128)(2,1)S(1)} %get-tuple-element.8.context_ref, f32[16,8,128]{2,1,0:T(8,128)S(1)} %bitcast.9, bf16[192,6144]{1,0:T(8,128)(2,1)S(1)} %copy-done, bf16[64,4096]{1,0:T(8,128)(2,1)S(1)} %copy-done.1), custom_call_target="tpu_custom_call" | custom-call | tf_op jit(solution)/shard_map/finish/pallas_call | solution.py:739
Async XLA Ops:
  0.6 111.1 %copy-start = (bf16[192,6144]{1,0:T(8,128)(2,1)S(1)}, bf16[192,6144]{1,0:T(8,128)(2,1)}, u32[]{:S(2)}) copy-start(bf16[192,6144]{1,0:T(8,128)(2,1)} %uq_ref.3) | copy-start | bytes 7077892
  0.6 111.1 %copy-start.1 = (bf16[64,4096]{1,0:T(8,128)(2,1)S(1)}, bf16[64,4096]{1,0:T(8,128)(2,1)}, u32[]{:S(2)}) copy-start(bf16[64,4096]{1,0:T(8,128)(2,1)} %uk_ref.3) | copy-start | bytes 1572868
